TPU v7x, 32 devices: a whole 2x2x4 slice. The times are simulated.
32 devices in a mesh: dp: 2 (over x), tp: 4 (over z), cp: 4 (over y, core).
Axes of the slice: x: 2, y: 2, z: 4, core: 2. Of those that a mesh axis runs over, the one named last changes fastest.
Arguments:
- hidden: bfloat16 [16, 64, 2560], P('dp'), parts along dimension 0
- prefix_len: int32 [16], P('dp'), parts along dimension 0
- k_cache: bfloat16 [16, 16384, 8, 128], P('dp', 'cp', 'tp'), parts along dimension 0
- v_cache: bfloat16 [16, 16384, 8, 128], P('dp', 'cp', 'tp'), parts along dimension 0
- attn_norm: bfloat16 [2560], replicated
- w_q: bfloat16 [2560, 4096], P(None, 'tp')
- w_k: bfloat16 [2560, 1024], P(None, 'tp')
- w_v: bfloat16 [2560, 1024], P(None, 'tp')
- w_o: bfloat16 [4096, 2560], P('tp')
- q_norm: bfloat16 [128], replicated
- k_norm: bfloat16 [128], replicated
Outputs:
- output 1: bfloat16 [16, 64, 2560], P('dp'), parts along dimension 0
- output 2: bfloat16 [16, 64, 8, 128], P('dp', None, 'tp'), parts along dimension 0
- output 3: bfloat16 [16, 64, 8, 128], P('dp', None, 'tp'), parts along dimension 0
There are 2 independent parts. A program takes and returns all parts, laid end to end along the dimension named above; an argument that names none is the same for every part.
All inputs are finite; a program needn't handle non-finite values.
Results may differ from a plain program's by a relative error of at most 0.00827889.
Values sent between devices are 32-bit elements.
A program may use at most 1 GiB of HBM per device.

v0:
```python
import jax
import jax.numpy as jnp
from jax import lax
from jax.sharding import PartitionSpec as P

HEAD_DIM = 128
MASKED = -1e30


def rms_scale(tensor, norm_gain):
    mean_sq = jnp.mean(jnp.square(tensor), axis=-1, keepdims=True)
    return tensor * lax.rsqrt(mean_sq + 1e-6) * norm_gain


def rope_apply(tensor, positions):
    half_dim = HEAD_DIM // 2
    inv_freq = 1.0 / (1000000.0 ** (jnp.arange(half_dim, dtype=jnp.float32) * 2.0 / HEAD_DIM))
    angles = positions.astype(jnp.float32)[..., None] * inv_freq
    cos_t = jnp.cos(angles)[..., None, :]
    sin_t = jnp.sin(angles)[..., None, :]
    lead_half = tensor[..., :half_dim]
    tail_half = tensor[..., half_dim:]
    return jnp.concatenate([lead_half * cos_t - tail_half * sin_t, tail_half * cos_t + lead_half * sin_t], axis=-1)


def project_new(hidden, attn_norm, w_q, w_k, w_v, q_norm, k_norm, prefix_len):
    n_seq, n_new, d_model = hidden.shape
    kv_count = w_k.shape[1] // HEAD_DIM
    head_count = w_q.shape[1] // HEAD_DIM
    normed = rms_scale(hidden.astype(jnp.float32), attn_norm.astype(jnp.float32)).astype(jnp.bfloat16)
    q_lin = jnp.einsum('bce,ef->bcf', normed, w_q, preferred_element_type=jnp.float32).astype(jnp.bfloat16)
    k_lin = jnp.einsum('bce,ef->bcf', normed, w_k, preferred_element_type=jnp.float32).astype(jnp.bfloat16)
    v_lin = jnp.einsum('bce,ef->bcf', normed, w_v, preferred_element_type=jnp.float32).astype(jnp.bfloat16)
    positions = prefix_len[:, None] + jnp.arange(n_new, dtype=jnp.int32)[None, :]
    q_heads = q_lin.reshape(n_seq, n_new, head_count, HEAD_DIM).astype(jnp.float32)
    k_heads = k_lin.reshape(n_seq, n_new, kv_count, HEAD_DIM).astype(jnp.float32)
    q_rot = rope_apply(rms_scale(q_heads, q_norm.astype(jnp.float32)), positions).astype(jnp.bfloat16)
    k_new = rope_apply(rms_scale(k_heads, k_norm.astype(jnp.float32)), positions).astype(jnp.bfloat16)
    v_new = v_lin.reshape(n_seq, n_new, kv_count, HEAD_DIM)
    q_grp = q_rot.reshape(n_seq, n_new, kv_count, head_count // kv_count, HEAD_DIM)
    return q_grp, k_new, v_new


def attend_partial(q_grp, k_cache, v_cache, k_new, v_new, slot_ok, own_ok):
    score_scale = HEAD_DIM ** -0.5
    s_cache = jnp.einsum('bckgd,bpkd->bkcgp', q_grp, k_cache, preferred_element_type=jnp.float32) * score_scale
    s_cache = jnp.where(slot_ok[:, None, None, None, :], s_cache, MASKED)
    s_own = jnp.einsum('bckgd,bikd->bkcgi', q_grp, k_new, preferred_element_type=jnp.float32) * score_scale
    s_own = jnp.where(own_ok[None, None, :, None, :], s_own, MASKED)
    row_max = jnp.maximum(jnp.max(s_cache, axis=-1), jnp.max(s_own, axis=-1))
    p_cache = jnp.exp(s_cache - row_max[..., None])
    p_own = jnp.exp(s_own - row_max[..., None])
    row_sum = jnp.sum(p_cache, axis=-1) + jnp.sum(p_own, axis=-1)
    weighted = jnp.einsum('bkcgp,bpkd->bkcgd', p_cache.astype(jnp.bfloat16), v_cache, preferred_element_type=jnp.float32)
    weighted = weighted + jnp.einsum('bkcgi,bikd->bkcgd', p_own.astype(jnp.bfloat16), v_new, preferred_element_type=jnp.float32)
    return row_max, row_sum, weighted


def out_partial(attn_out, w_o):
    kv_count = attn_out.shape[1]
    group_size = attn_out.shape[3]
    w_heads = w_o.reshape(kv_count, group_size, HEAD_DIM, w_o.shape[1])
    return jnp.einsum('bkcgd,kgde->bce', attn_out, w_heads, preferred_element_type=jnp.float32)


def solution(mesh):
    def per_device(hidden, prefix_len, k_cache, v_cache, attn_norm, w_q, w_k, w_v, w_o, q_norm, k_norm):
        n_new = hidden.shape[1]
        cache_slots = k_cache.shape[1]
        cp_index = lax.axis_index('cp')
        q_grp, k_new, v_new = project_new(hidden, attn_norm, w_q, w_k, w_v, q_norm, k_norm, prefix_len)
        slot_ids = cp_index * cache_slots + jnp.arange(cache_slots)
        slot_ok = slot_ids[None, :] < prefix_len[:, None]
        new_ids = jnp.arange(n_new)
        own_ok = (new_ids[:, None] >= new_ids[None, :]) & (cp_index == 0)
        row_max, row_sum, weighted = attend_partial(q_grp, k_cache, v_cache, k_new, v_new, slot_ok, own_ok)
        glob_max = lax.pmax(row_max, 'cp')
        factor = jnp.exp(row_max - glob_max)
        total_w, total_sum = lax.psum((weighted * factor[..., None], row_sum * factor), 'cp')
        attn_out = (total_w / total_sum[..., None]).astype(jnp.bfloat16)
        out_proj = lax.psum(out_partial(attn_out, w_o), 'tp')
        block_out = (hidden.astype(jnp.float32) + out_proj).astype(jnp.bfloat16)
        return block_out, k_new, v_new

    cache_spec = P('dp', 'cp', 'tp', None)
    arg_specs = (P('dp', None, None), P('dp'), cache_spec, cache_spec, P(None), P(None, 'tp'), P(None, 'tp'), P(None, 'tp'), P('tp', None), P(None), P(None))
    out_specs = (P('dp', None, None), P('dp', None, 'tp', None), P('dp', None, 'tp', None))
    return jax.shard_map(per_device, mesh=mesh, in_specs=arg_specs, out_specs=out_specs, check_vma=False)
```

profile of v0, /device:TPU:0, one launch (start us, length us, event | category | flops | bytes accessed | tf_op | source)
XLA Modules:
  0.0 395.3 jit_solution(2813162845524200175)
XLA Ops:
  7.3 0.8 convert_element_type.61
  8.1 2.6 fusion.8
  10.7 0.9 fusion.43
  11.7 0.3 reshape.129
  12.0 0.6 multiply_reduce_fusion
  12.8 5.8 %fusion.28 = f32[8,64,1024]{2,1,0:T(8,128)S(1)} fusion(bf16[2560,1024]{1,0:T(8,128)(2,1)} %param.16, bf16[8,64,2560]{2,1,0:T(8,128)(2,1)} %param.11, f32[2560]{0:T(1024)S(1)} %convert_element_type.61, f32[8,64]{1,0:T(8,128)S(1)} %add_rsqrt_fusion.2), kind=kOutput, calls=%fused_computation.37 | convolution fusion | flops 2690646016 | bytes 9973760 | tf_op jit(solution)/shard_map/bce,ef->bcf/dot_general | solution.py:31
  18.7 0.5 copy.81
  19.2 0.6 fusion.20
  20.3 1.0 multiply_cosine_fusion
  21.3 1.0 subtract_convert_fusion.1
  22.3 0.7 fusion.21
  23.0 0.9 subtract_convert_fusion
  24.0 0.3 copy.49
  24.2 0.3 copy.50
  24.7 0.2 copy-done.9
  25.1 0.7 copy-done.5
  25.8 2.6 fusion.22
  28.4 30.0 %fusion = (f32[8,2,64,4]{2,3,1,0:T(4,128)S(1)}, f32[8,2,64,4,4096]{4,2,3,1,0:T(8,128)}) fusion(pred[8,4096]{1,0:T(8,128)(4,1)S(1)} %broadcast_compare_fusion, bf16[8,4096,2,128,1]{3,2,1,0,4:T(2,128)(2,1)} %bitcast.72, bf16[8,64,2,4,64]{4,1,3,2,0:T(8,128)(2,1)S(1)} %bitcast.76, bf16[8,64,2,4,64]{4,1,3,2,0:T(8,128)(2,1)S(1)} %bitcast.74), kind=kOutput, calls=%fused_computation.2 | convolution fusion | flops 4347392000 | bytes 84983808 | tf_op jit(solution)/shard_map/bckgd,bpkd->bkcgp/dot_general | solution.py:46
  58.4 13.0 %pmax.7 = f32[8,2,64,4]{2,3,1,0:T(4,128)S(1)} all-reduce(f32[8,2,64,4]{2,3,1,0:T(4,128)S(1)} %max.9), channel_id=1, replica_groups=mesh['dp'=2,'tp'=4,'cp'=4] {'cp'}, use_global_device_ids=true, to_apply=%region_5.6 | all-reduce | flops 4096 | bytes 32768 | tf_op jit(solution)/shard_map/pmax | solution.py:77
  71.5 33.6 %fusion.1 = (f32[8,2,64,4]{2,3,1,0:T(4,128)S(1)}, bf16[8,2,64,4,4096]{4,2,3,1,0:T(8,128)(2,1)}) fusion(f32[8,2,64,4,4096]{4,2,3,1,0:T(8,128)} %get-tuple-element.28, f32[8,2,64,4]{2,3,1,0:T(4,128)S(1)} %max.9, pred[8,4096]{1,0:T(8,128)(4,1)S(1)} %broadcast_compare_fusion), kind=kLoop, calls=%fused_computation.3 | loop fusion | flops 83881984 | bytes 100728832 | tf_op jit(solution)/shard_map/reduce_sum | solution.py:53
  105.1 0.7 fusion.23
  105.9 0.9 copy-done.3
  106.8 2.2 fusion.48
  109.1 24.1 %fusion.3 = f32[8,2,64,4,128]{4,2,1,3,0:T(8,128)S(1)} fusion(bf16[8,2,64,4,4096]{4,2,3,1,0:T(8,128)(2,1)} %get-tuple-element.18, bf16[8,4096,2,128,1]{3,2,1,0,4:T(2,128)(2,1)} %bitcast.85), kind=kOutput, calls=%fused_computation.5 | convolution fusion | flops 4294967296 | bytes 52428800 | tf_op jit(solution)/shard_map/bkcgp,bpkd->bkcgd/dot_general | solution.py:54
  133.3 2.0 add_multiply_fusion
  135.4 11.1 %psum.22 = f32[8,2,64,4]{2,3,1,0:T(4,128)S(1)} all-reduce(f32[8,2,64,4]{2,3,1,0:T(4,128)S(1)} %bitcast.82), channel_id=1, replica_groups=mesh['dp'=2,'tp'=4,'cp'=4] {'cp'}, use_global_device_ids=true, to_apply=%region_9.10 | all-reduce | flops 4096 | bytes 32768 | tf_op jit(solution)/shard_map/psum | solution.py:79
  146.5 40.7 %all-reduce.3.cloned.1.call-done = f32[8,2,64,4,128]{4,2,1,3,0:T(8,128)} async-done(((f32[8,2,64,4,128]{4,2,1,3,0:T(8,128)}), f32[8,2,64,4,128]{4,2,1,3,0:T(8,128)}) %all-reduce.3.cloned.1.call-update) | async-done | bytes 2097168 | tf_op jit(solution)/shard_map/psum | solution.py:79
  187.2 7.6 %fusion.17 = f32[8,64,2560]{2,1,0:T(8,128)} fusion(bf16[2,4,128,2560,1]{3,2,1,0,4:T(8,128)(2,1)} %bitcast.86, f32[8,2,64,4,128]{4,2,1,3,0:T(8,128)} %all-reduce.3.cloned.1.call-done, f32[8,2,64,4]{2,1,3,0:T(2,128)S(1)} %copy.60), kind=kOutput, calls=%fused_computation.22 | convolution fusion | flops 2685403136 | bytes 12599296 | tf_op jit(solution)/shard_map/bkcgd,kgde->bce/dot_general | solution.py:63
  194.8 0.9 copy-done.6
  195.7 1.0 copy.63
  196.7 186.2 %all-reduce.5.cloned.1.call-done = f32[8,64,2560]{2,1,0:T(8,128)} async-done(((f32[8,64,2560]{2,1,0:T(8,128)}), f32[8,64,2560]{2,1,0:T(8,128)}) %all-reduce.5.cloned.1.call-update) | async-done | bytes 5242896 | tf_op jit(solution)/shard_map/psum | solution.py:81
  382.8 5.6 %fusion.11 = bf16[8,64,2560]{2,1,0:T(8,128)(2,1)} fusion(f32[8,64,2560]{2,1,0:T(8,128)} %all-reduce.5.cloned.1.call-done, bf16[8,64,2560]{2,1,0:T(8,128)(2,1)} %param.11), kind=kLoop, calls=%fused_computation.16 | loop fusion | flops 3932160 | bytes 10485760 | tf_op jit(solution)/shard_map/convert_element_type | solution.py:82
  (51 shorter events, 1.4 us)
Async XLA Ops:
  7.2 3.5 copy-start
  7.2 180.0 %all-reduce.3.cloned.1.call-start = ((), (), s32[]{:S(2)}) async-start(), calls=%async_computation | async-start | bytes 4194304 | tf_op jit(solution)/shard_map/psum | solution.py:79
  7.2 3.5 copy-start.2
  10.7 2.0 copy-start.13
  10.7 2.0 copy-start.12
  11.7 7.0 %copy-start.7 = (f32[8,64,256]{2,1,0:T(8,128)}, f32[8,64,256]{2,1,0:T(8,128)S(1)}, u32[]{:S(2)}) copy-start(f32[8,64,256]{2,1,0:T(8,128)S(1)} %fusion.43) | copy-start | bytes 1572868
  18.7 1.4 copy-start.14
  18.7 1.4 copy-start.8
  23.9 1.0 copy-start.9
  24.0 1.0 copy-start.10
  25.1 0.7 copy-start.5
  71.4 33.7 %copy-start.4 = (f32[8,2,64,4,64]{2,4,3,1,0:T(8,128)S(1)}, f32[8,2,64,4,64]{2,4,3,1,0:T(8,128)}, u32[]{:S(2)}) copy-start(f32[8,2,64,4,64]{2,4,3,1,0:T(8,128)} %get-tuple-element.30) | copy-start | bytes 3145732
  105.1 1.7 copy-start.3
  109.1 24.1 %copy-start.11 = (bf16[8,64,2,128]{3,2,1,0:T(2,128)(2,1)}, bf16[8,64,2,128]{3,2,1,0:T(2,128)(2,1)S(1)}, u32[]{:S(2)}) copy-start(bf16[8,64,2,128]{3,2,1,0:T(2,128)(2,1)S(1)} %reshape.126) | copy-start | bytes 786436
  135.3 247.5 %all-reduce.5.cloned.1.call-start = ((), (), s32[]{:S(2)}) async-start(), calls=%async_computation.1 | async-start | bytes 10485760 | tf_op jit(solution)/shard_map/psum | solution.py:81
  194.8 0.9 copy-start.6
  382.8 5.6 %copy-start.1 = (bf16[2560,256]{1,0:T(8,128)(2,1)S(1)}, bf16[2560,256]{1,0:T(8,128)(2,1)}, u32[]{:S(2)}) copy-start(bf16[2560,256]{1,0:T(8,128)(2,1)} %param.17) | copy-start | bytes 3932164
Sparse Core Ops, SparseCore 0:
  135.4 51.7 all-reduce.2
  194.9 187.8 all-reduce.4
where the time goes:
time: 396 us; the launch traced here: 395 us
  waiting for transfers between devices  227 us (57%)
  matrix products  75.2 us (19%)
  other arithmetic  48.9 us (12%)
  blocking collectives  24.1 us (6%)
  between operations  14.4 us (4%)
  local copies, waits for them, and re-layouts  5.67 us (1%)
    psum x1, waiting for transfers between devices, per_device(): out_proj = lax.psum(out_partial(attn_out, w_o), 'tp')  186 us
    psum x1, waiting for transfers between devices, per_device(): lax.psum((weighted * factor[..., None], row_sum * factor), 'cp')  40.7 us
    reduce_sum x2, other arithmetic, attend_partial(): row_sum = jnp.sum(p_cache, axis=-1) + jnp.sum(p_own, axis=-1)  34.4 us
    dot_general x1, matrix products, attend_partial(): jnp.einsum('bckgd,bpkd->bkcgp', q_grp, k_cache, preferred_element_type=jn...  30 us
    dot_general x1, matrix products, attend_partial(): jnp.einsum('bkcgp,bpkd->bkcgd', p_cache.astype(jnp.bfloat16), v_cache, pr...  24.1 us
    pmax x1, blocking collectives, per_device(): glob_max = lax.pmax(row_max, 'cp')  13 us
    psum x1, blocking collectives, per_device(): lax.psum((weighted * factor[..., None], row_sum * factor), 'cp')  11.1 us
  transfers between devices with their start and end apart: 2, of which 2 were waited for; matrix products, arithmetic and copies ran while one was open for 0% of the time, Pallas kernels for 0%

commit v1 on v0

v1 whole, which is shorter than its diff:
```python
import functools

import jax
import jax.numpy as jnp
import numpy as np
from jax import lax
from jax.experimental import pallas as pl
from jax.experimental.pallas import tpu as pltpu
from jax.sharding import PartitionSpec as P

HEAD_DIM = 128
MASKED = -1e30
EPS = 1e-6
LOG2_SCALE = float(HEAD_DIM ** -0.5 / np.log(2.0))
MESH = pl.DeviceIdType.MESH
NT = (((1,), (1,)), ((), ()))
TN = (((0,), (0,)), ((), ()))
F32 = jnp.float32
BF16 = jnp.bfloat16


def project_kernel(prefix_ref, x_ref, an_ref, wq_hbm, wk_hbm, wv_hbm, qn_ref, kn_ref, freq_ref,
                   q_ref, k_ref, v_ref, wq, wk, wv, normed, cos_ref, sin_ref, sems):
    n_seq, n_new = k_ref.shape[0], k_ref.shape[2]
    rows = n_seq * n_new
    copies = [pltpu.make_async_copy(wq_hbm.at[:, pl.ds(256 * j, 256)], wq.at[j], sems.at[j]) for j in range(4)]
    copies.append(pltpu.make_async_copy(wk_hbm, wk, sems.at[4]))
    copies.append(pltpu.make_async_copy(wv_hbm, wv, sems.at[5]))
    for c in copies:
        c.start()
    for r in range(0, rows, 64):
        x = x_ref[r:r + 64, :].astype(F32)
        scale = lax.rsqrt(jnp.mean(x * x, axis=-1, keepdims=True) + EPS)
        normed[r:r + 64, :] = (x * scale * an_ref[...].astype(F32)).astype(BF16)
    lane = lax.broadcasted_iota(jnp.int32, (n_new, HEAD_DIM), 1)
    step = lax.broadcasted_iota(jnp.int32, (n_new, HEAD_DIM), 0)
    for b in range(n_seq):
        angle = (prefix_ref[b] + step).astype(F32) * freq_ref[...]
        cos_ref[b * n_new:(b + 1) * n_new, :] = jnp.cos(angle)
        sin_t = jnp.sin(angle)
        sin_ref[b * n_new:(b + 1) * n_new, :] = jnp.where(lane < HEAD_DIM // 2, -sin_t, sin_t)

    def norm_rope(y, gain_ref):
        y = y.astype(BF16).astype(F32)
        y = y * lax.rsqrt(jnp.mean(y * y, axis=-1, keepdims=True) + EPS) * gain_ref[...].astype(F32)
        return (y * cos_ref[...] + pltpu.roll(y, HEAD_DIM // 2, 1) * sin_ref[...]).astype(BF16)

    for j in range(4):
        copies[j].wait()
        y = jnp.dot(normed[...], wq[j], preferred_element_type=F32)
        for i in range(2):
            h, g = j // 2, 2 * (j % 2) + i
            head = norm_rope(y[:, i * HEAD_DIM:(i + 1) * HEAD_DIM], qn_ref)
            for b in range(n_seq):
                for c in range(2):
                    q_ref[b, c * 128 + g * 32:c * 128 + g * 32 + 32, h * 128:(h + 1) * 128] = (
                        head[b * 64 + c * 32:b * 64 + c * 32 + 32])
    copies[4].wait()
    y = jnp.dot(normed[...], wk[...], preferred_element_type=F32)
    for h in range(2):
        head = norm_rope(y[:, h * HEAD_DIM:(h + 1) * HEAD_DIM], kn_ref)
        for b in range(n_seq):
            k_ref[b, h] = head[b * 64:(b + 1) * 64]
    copies[5].wait()
    y = jnp.dot(normed[...], wv[...], preferred_element_type=F32).astype(BF16)
    for h in range(2):
        for b in range(n_seq):
            v_ref[b, h] = y[b * 64:(b + 1) * 64, h * HEAD_DIM:(h + 1) * HEAD_DIM]


def project(hidden, prefix_len, attn_norm, w_q, w_k, w_v, q_norm, k_norm):
    n_seq, n_new, d_model = hidden.shape
    freq = 1.0 / (1000000.0 ** (np.arange(HEAD_DIM // 2, dtype=np.float64) * 2.0 / HEAD_DIM))
    freq = jnp.asarray(np.concatenate([freq, freq])[None].astype(np.float32))
    vmem = pl.BlockSpec(memory_space=pltpu.VMEM)
    hbm = pl.BlockSpec(memory_space=pl.ANY)
    rows = n_seq * n_new
    return pl.pallas_call(
        project_kernel,
        out_shape=(jax.ShapeDtypeStruct((n_seq, 256, 256), BF16),
                   jax.ShapeDtypeStruct((n_seq, 2, n_new, HEAD_DIM), BF16),
                   jax.ShapeDtypeStruct((n_seq, 2, n_new, HEAD_DIM), BF16)),
        in_specs=[pl.BlockSpec(memory_space=pltpu.SMEM), vmem, vmem, hbm, hbm, hbm, vmem, vmem, vmem],
        out_specs=(vmem, vmem, vmem),
        scratch_shapes=[pltpu.VMEM((4, d_model, 256), BF16), pltpu.VMEM((d_model, 256), BF16),
                        pltpu.VMEM((d_model, 256), BF16), pltpu.VMEM((rows, d_model), BF16),
                        pltpu.VMEM((rows, HEAD_DIM), F32), pltpu.VMEM((rows, HEAD_DIM), F32),
                        pltpu.SemaphoreType.DMA((6,))],
        compiler_params=pltpu.CompilerParams(vmem_limit_bytes=48 << 20),
        cost_estimate=pl.CostEstimate(flops=2 * rows * d_model * 1536, bytes_accessed=12 << 20, transcendentals=0),
        name="project",
    )(prefix_len, hidden.reshape(rows, d_model), attn_norm[None], w_q, w_k, w_v, q_norm[None], k_norm[None], freq)


def pair_reduce(op, x):
    x = op(x, pltpu.roll(x, 2, 0))
    return op(x, pltpu.roll(x, 4, 0))


def own_keys(q, k_own_ref, v_own_ref, first):
    n_new = k_own_ref.shape[-2]
    key = lax.broadcasted_iota(jnp.int32, (n_new, 256), 0)
    col = lax.broadcasted_iota(jnp.int32, (n_new, 256), 1)
    token = (col // 128) * 32 + col % 32
    keep = jnp.logical_and(key <= token, first)
    maxes, sums, accs = [], [], []
    for h in range(2):
        s = lax.dot_general(k_own_ref[h], q[:, h * 128:(h + 1) * 128], NT, preferred_element_type=F32)
        s = jnp.where(keep, s * LOG2_SCALE, MASKED)
        m = jnp.max(s, axis=0, keepdims=True)
        p = jnp.exp2(s - m)
        maxes.append(m)
        sums.append(jnp.sum(p, axis=0, keepdims=True))
        accs.append(lax.dot_general(v_own_ref[h], p.astype(BF16), TN, preferred_element_type=F32))
    even = lax.broadcasted_iota(jnp.int32, (8, 256), 0) % 2 == 0
    return (jnp.where(even, maxes[0], maxes[1]), jnp.where(even, sums[0], sums[1]), accs)


def block_scores(q, k_ref, s_ref, row0, limit, step=512):
    rows = k_ref.shape[0]
    even = (lax.broadcasted_iota(jnp.int32, (step, HEAD_DIM), 0) % 2 == 0)
    even_f = even.astype(F32).astype(BF16)
    odd_f = (1.0 - even.astype(F32)).astype(BF16)
    row = lax.broadcasted_iota(jnp.int32, (step, 256), 0)
    block_max = jnp.full((8, 256), MASKED, F32)
    for r in range(0, rows, step):
        k = k_ref[r:r + step, :]
        both = jnp.concatenate([k * even_f, k * odd_f], axis=1)
        s = lax.dot_general(both, q, NT, preferred_element_type=F32)
        s = jnp.where(row < limit - (row0 + r), s, MASKED)
        s_ref[r:r + step, :] = s
        block_max = jnp.maximum(block_max, jnp.max(s.reshape(step // 8, 8, 256), axis=0))
    return pair_reduce(jnp.maximum, block_max)


def block_values(v_ref, s_ref, m8, step=1024):
    rows = v_ref.shape[0]
    even = (lax.broadcasted_iota(jnp.int32, (HEAD_DIM, step), 1) % 2 == 0)
    even_f = even.astype(F32).astype(BF16)
    odd_f = (1.0 - even.astype(F32)).astype(BF16)
    l8 = jnp.zeros((8, 256), F32)
    acc = None
    for r in range(0, rows, step):
        p = jnp.exp2(s_ref[r:r + step, :].reshape(step // 8, 8, 256) * LOG2_SCALE - m8[None])
        l8 = l8 + jnp.sum(p, axis=0)
        vt = v_ref[r:r + step, :].T
        both = jnp.concatenate([vt * even_f, vt * odd_f], axis=0)
        part = jnp.dot(both, p.reshape(step, 256).astype(BF16), preferred_element_type=F32)
        acc = part if acc is None else acc + part
    return pair_reduce(jnp.add, l8), acc


def attend_kernel(prefix_ref, q_ref, k_ref, v_ref, k_own, v_own, o_ref, s_ref, m_ref, l_ref, acc_ref):
    b, j = pl.program_id(0), pl.program_id(1)
    rows = k_ref.shape[1]
    cp = lax.axis_index("cp")
    limit = 2 * prefix_ref[b] - cp * (rows * pl.num_programs(1))
    q = q_ref[0]

    @pl.when(j == 0)
    def _():
        m8, l8, accs = own_keys(q, k_own.at[0], v_own.at[0], cp == 0)
        m_ref[...] = m8
        l_ref[...] = l8
        for h in range(2):
            acc_ref[h * 128:(h + 1) * 128, :] = accs[h]

    @pl.when(j * rows < limit)
    def _():
        block_max = block_scores(q, k_ref.at[0], s_ref, j * rows, limit)
        m8 = jnp.maximum(m_ref[...], block_max * LOG2_SCALE)
        alpha = jnp.exp2(m_ref[...] - m8)
        l8, acc = block_values(v_ref.at[0], s_ref, m8)
        m_ref[...] = m8
        l_ref[...] = l_ref[...] * alpha + l8
        for h in range(2):
            part = slice(h * 128, (h + 1) * 128)
            acc_ref[part, :] = acc_ref[part, :] * alpha[h:h + 1] + acc[part]

    @pl.when(j == pl.num_programs(1) - 1)
    def _():
        sub = lax.broadcasted_iota(jnp.int32, (8, 256), 0)
        stats = jnp.where(sub < 2, m_ref[...], l_ref[...])
        for c in range(2):
            o_ref[0, c, 0:256, :] = acc_ref[:, c * 128:(c + 1) * 128]
            o_ref[0, c, 256:264, :] = stats[:, c * 128:(c + 1) * 128]


def attend(prefix_len, q, k_cache, v_cache, k_own, v_own):
    n_seq, slots = k_cache.shape[0], k_cache.shape[1]
    rows = 4096
    n_new = k_own.shape[2]
    k_rows = k_cache.reshape(n_seq, slots * 2, HEAD_DIM)
    v_rows = v_cache.reshape(n_seq, slots * 2, HEAD_DIM)
    blocks = slots * 2 // rows
    cache_spec = pl.BlockSpec((1, rows, HEAD_DIM), lambda b, j: (b, j, 0))
    own_spec = pl.BlockSpec((1, 2, n_new, HEAD_DIM), lambda b, j: (b, 0, 0, 0))
    return pl.pallas_call(
        attend_kernel,
        grid=(n_seq, blocks),
        out_shape=jax.ShapeDtypeStruct((n_seq, 2, 264, 128), F32),
        in_specs=[pl.BlockSpec(memory_space=pltpu.SMEM), pl.BlockSpec((1, 256, 256), lambda b, j: (b, 0, 0)),
                  cache_spec, cache_spec, own_spec, own_spec],
        out_specs=pl.BlockSpec((1, 2, 264, 128), lambda b, j: (b, 0, 0, 0)),
        scratch_shapes=[pltpu.VMEM((rows, 256), F32), pltpu.VMEM((8, 256), F32), pltpu.VMEM((8, 256), F32),
                        pltpu.VMEM((256, 256), F32)],
        compiler_params=pltpu.CompilerParams(vmem_limit_bytes=40 << 20),
        cost_estimate=pl.CostEstimate(flops=17 << 30, bytes_accessed=36 << 20, transcendentals=17 << 20),
        name="attend",
    )(prefix_len, q, k_rows, v_rows, k_own, v_own)


def merge(parts):
    sub = lax.broadcasted_iota(jnp.int32, (8, 128), 0)
    stats = [p[256:264, :] for p in parts]
    maxes = [jnp.where(sub % 4 < 2, s, pltpu.roll(s, 2, 0)) for s in stats]
    top = functools.reduce(jnp.maximum, maxes)
    weights = [jnp.exp2(m - top) for m in maxes]
    total = sum(w * s for w, s in zip(weights, stats))
    stats_out = jnp.where(sub < 2, top, total)
    accs = [sum(w[h:h + 1] * p[h * 128:(h + 1) * 128, :] for w, p in zip(weights, parts)) for h in range(2)]
    return accs, stats_out


def combine_kernel(part_ref, x_hbm, wo_hbm, out_ref, x_buf, wo, ra1, sa2, ra2, proj, rs_o, rs_i, fwd, og,
                   loc_sem, a1_s, a1_r, a2_s, a2_r, rs_s, rso_r, rsi_r, og_s, og_r):
    n_seq = part_ref.shape[0]
    units = n_seq // 2
    half_cols = proj.shape[-1]
    cp, z = lax.axis_index("cp"), lax.axis_index("tp")
    y, c = cp // 2, cp % 2
    is_mid = jnp.logical_and(z >= 1, z <= 2)
    is_end = jnp.logical_not(is_mid)
    near, far = z // 2, 1 - z // 2
    outer = jnp.where(z == 1, 0, 3)
    inner = jnp.where(z == 1, 2, 1)
    mid = jnp.where(z == 0, 1, 2)
    core_peer = {"cp": y * 2 + 1 - c}
    y_peer = {"cp": (1 - y) * 2 + c}
    me, yq = y * 2 + c, (1 - y) * 2 + c

    def remote(src, dst, send_sem, recv_sem, peer):
        return pltpu.make_async_remote_copy(src_ref=src, dst_ref=dst, send_sem=send_sem, recv_sem=recv_sem,
                                            device_id=peer, device_id_type=MESH)

    wo_copy = pltpu.make_async_copy(wo_hbm, wo, loc_sem.at[0])
    wo_copy.start()
    x_copies = [pltpu.make_async_copy(x_hbm.at[2 * u + y, pl.ds(32 * c, 32), :], x_buf.at[u], loc_sem.at[1 + u])
                for u in range(units)]
    for x_copy in x_copies:
        x_copy.start()

    barrier = pltpu.get_barrier_semaphore()
    pl.semaphore_signal(barrier, inc=1, device_id=core_peer, device_id_type=MESH)
    pl.semaphore_signal(barrier, inc=1, device_id=y_peer, device_id_type=MESH)

    @pl.when(is_mid)
    def _():
        pl.semaphore_signal(barrier, inc=1, device_id={"tp": outer}, device_id_type=MESH)
        pl.semaphore_signal(barrier, inc=1, device_id={"tp": inner}, device_id_type=MESH)
        pl.semaphore_wait(barrier, 4)

    @pl.when(is_end)
    def _():
        pl.semaphore_signal(barrier, inc=1, device_id={"tp": mid}, device_id_type=MESH)
        pl.semaphore_wait(barrier, 3)

    def a1(b):
        return remote(part_ref.at[b, 1 - c], ra1.at[b], a1_s.at[b], a1_r.at[b], core_peer)

    def a2(u):
        return remote(sa2.at[u], ra2.at[u], a2_s.at[u], a2_r.at[u], y_peer)

    def rs_out(u, half):
        return remote(proj.at[u, half], rs_o.at[u, half], rs_s.at[u, half], rso_r.at[u, half], {"tp": mid})

    def rs_in(u):
        return remote(fwd.at[u], rs_i.at[u], rs_s.at[u, 0], rsi_r.at[u], {"tp": inner})

    def gather(q, u, half, lane, peer):
        return remote(og.at[q, u, half], og.at[q, u, half], og_s.at[lane, u, half], og_r.at[q, u, half], peer)

    for b in range(n_seq):
        a1(b).start()

    def s1(u):
        b = 2 * u + 1 - y
        a1(b).wait_recv()
        accs, stats = merge([part_ref[b, c], ra1[b]])
        for h in range(2):
            sa2[u, h * 128:(h + 1) * 128, :] = accs[h]
        sa2[u, 256:264, :] = stats
        a2(u).start()

    def s2(u):
        b = 2 * u + y
        a1(b).wait_recv()
        a2(u).wait_recv()
        accs, stats = merge([part_ref[b, c], ra1[b], ra2[u]])
        heads = []
        for h in range(2):
            o = (accs[h] / stats[2 + h:3 + h]).T.astype(BF16)
            heads += [o[g * 32:(g + 1) * 32] for g in range(4)]
        o = jnp.concatenate(heads, axis=1)
        for half in range(2):
            proj[u, half] = jnp.dot(o, wo[:, half * half_cols:(half + 1) * half_cols], preferred_element_type=F32)

        @pl.when(is_end)
        def _():
            rs_out(u, far).start()
            rs_out(u, near).start()

    def s3(u):
        @pl.when(is_mid)
        def _():
            rs_out(u, far).wait_recv()
            fwd[u] = proj[u, far] + rs_o[u, far]
            rs_in(u).start()

    def x_half(u):
        lo = x_buf[u, :, 0:half_cols].astype(F32)
        hi = x_buf[u, :, half_cols:2 * half_cols].astype(F32)
        return jnp.where(near == 0, lo, hi)

    def s4(u):
        @pl.when(is_mid)
        def _():
            rs_out(u, near).wait_recv()
            rs_in(u).wait_recv()
            total = (proj[u, near] + rs_o[u, near]) + rs_i[u]
            og[me, u, near] = (x_half(u) + total).astype(BF16).astype(F32)
            gather(me, u, near, 2, {"tp": inner}).start()
            gather(me, u, near, 3, {"tp": outer}).start()

        @pl.when(is_end)
        def _():
            gather(me, u, near, 2, {"tp": mid}).wait_recv()

        gather(me, u, near, 1, y_peer).start()
        gather(me, u, near, 0, core_peer).start()

    def s5(u):
        gather(me, u, far, 2, {"tp": inner}).wait_recv()

        @pl.when(is_mid)
        def _():
            gather(me, u, far, 3, {"tp": outer}).start()

        gather(me, u, far, 1, y_peer).start()
        gather(me, u, far, 0, core_peer).start()

    def s6(u):
        for half in (near, far):
            gather(yq, u, half, 1, y_peer).wait_recv()
            gather(yq, u, half, 4, core_peer).start()

    def s7(u):
        for q in (y * 2 + 1 - c, (1 - y) * 2 + 1 - c):
            for half in range(2):
                gather(q, u, half, 0, core_peer).wait_recv()
        for q in range(4):
            for half in range(2):
                out_ref[2 * u + q // 2, 32 * (q % 2):32 * (q % 2) + 32, half * half_cols:(half + 1) * half_cols] = (
                    og[q, u, half].astype(BF16))

    wo_copy.wait()
    for x_copy in x_copies:
        x_copy.wait()
    stages = (s1, s2, s3, s4, s5, s6, s7)

    def slot(t, carry):
        for i, stage in enumerate(stages):
            @pl.when(jnp.logical_and(t >= i, t < units + i))
            def _(stage=stage, i=i):
                stage(t - i)
        return carry

    lax.fori_loop(0, units + len(stages) - 1, slot, 0)

    for b in range(n_seq):
        a1(b).wait_send()
    for u in range(units):
        a2(u).wait_send()
        for half in (near, far):
            gather(me, u, half, 0, core_peer).wait_send()
            gather(me, u, half, 1, y_peer).wait_send()
            gather(yq, u, half, 4, core_peer).wait_send()

    @pl.when(is_end)
    def _():
        for u in range(units):
            for half in (near, far):
                rs_out(u, half).wait_send()

    @pl.when(is_mid)
    def _():
        for u in range(units):
            rs_in(u).wait_send()
            gather(me, u, near, 2, {"tp": inner}).wait_send()
            for half in (near, far):
                gather(me, u, half, 3, {"tp": outer}).wait_send()


def combine(parts, hidden, w_o):
    n_seq, n_new, d_model = hidden.shape
    units, half = n_seq // 2, d_model // 2
    vmem = pl.BlockSpec(memory_space=pltpu.VMEM)
    hbm = pl.BlockSpec(memory_space=pl.ANY)
    dma = pltpu.SemaphoreType.DMA
    return pl.pallas_call(
        combine_kernel,
        out_shape=jax.ShapeDtypeStruct((n_seq, n_new, d_model), BF16),
        in_specs=[vmem, hbm, hbm],
        out_specs=vmem,
        scratch_shapes=[
            pltpu.VMEM((units, 32, d_model), BF16), pltpu.VMEM(w_o.shape, BF16),
            pltpu.VMEM((n_seq, 264, 128), F32), pltpu.VMEM((units, 264, 128), F32),
            pltpu.VMEM((units, 264, 128), F32), pltpu.VMEM((units, 2, 32, half), F32),
            pltpu.VMEM((units, 2, 32, half), F32), pltpu.VMEM((units, 32, half), F32),
            pltpu.VMEM((units, 32, half), F32), pltpu.VMEM((4, units, 2, 32, half), F32),
            dma((1 + units,)), dma((n_seq,)), dma((n_seq,)), dma((units,)), dma((units,)), dma((units, 2)),
            dma((units, 2)), dma((units,)), dma((5, units, 2)), dma((4, units, 2))],
        compiler_params=pltpu.CompilerParams(collective_id=0, has_side_effects=True, vmem_limit_bytes=48 << 20),
        cost_estimate=pl.CostEstimate(flops=2 << 30, bytes_accessed=10 << 20, transcendentals=0),
        name="combine",
    )(parts, hidden, w_o)


def solution(mesh):
    def per_device(hidden, prefix_len, k_cache, v_cache, attn_norm, w_q, w_k, w_v, w_o, q_norm, k_norm):
        q, k_own, v_own = project(hidden, prefix_len, attn_norm, w_q, w_k, w_v, q_norm, k_norm)
        parts = attend(prefix_len, q, k_cache, v_cache, k_own, v_own)
        block_out = combine(parts, hidden, w_o)
        return block_out, k_own.transpose(0, 2, 1, 3), v_own.transpose(0, 2, 1, 3)

    cache_spec = P('dp', 'cp', 'tp', None)
    arg_specs = (P('dp', None, None), P('dp'), cache_spec, cache_spec, P(None), P(None, 'tp'), P(None, 'tp'), P(None, 'tp'), P('tp', None), P(None), P(None))
    out_specs = (P('dp', None, None), P('dp', None, 'tp', None), P('dp', None, 'tp', None))
    return jax.shard_map(per_device, mesh=mesh, in_specs=arg_specs, out_specs=out_specs, check_vma=False)
```

time: 396 us -> 145 us (0.37)
  waiting for transfers between devices: 227 us -> 0 us
  Pallas kernels: 0 us -> 135 us
  matrix products: 75.2 us -> 0 us
  other arithmetic: 48.9 us -> 0 us
  blocking collectives: 24.1 us -> 0 us
  between operations: 14.4 us -> 0.67 us
    psum x2 -> x0, waiting for transfers between devices: 227 us -> none  [the longest x1 186 us: per_device(): out_proj = lax.psum(out_partial(attn_out, w_o), 'tp')]
    pallas_call x0 -> x3, Pallas kernels: none -> 135 us  [the longest x1 64.5 us: combine(): pl.pallas_call(combine_kernel, out_shape=jax.ShapeDtypeStruct((n_seq, n_n...]
    dot_general x8 -> x0, matrix products: 75.2 us -> none  [the longest x1 30 us: attend_partial(): jnp.einsum('bckgd,bpkd->bkcgp', q_grp, k_cache, preferred_element_type=jn...]
    reduce_sum x5 -> x0, other arithmetic: 38.2 us -> none  [the longest x2 34.4 us: attend_partial(): row_sum = jnp.sum(p_cache, axis=-1) + jnp.sum(p_own, axis=-1)]
    pmax x1 -> x0, blocking collectives: 13 us -> none  [per_device(): glob_max = lax.pmax(row_max, 'cp')]
    psum x1 -> x0, blocking collectives: 11.1 us -> none  [per_device(): lax.psum((weighted * factor[..., None], row_sum * factor), 'cp')]
    convert_element_type x5 -> x0, other arithmetic: 6.57 us -> none  [the longest x1 5.64 us: per_device(): block_out = (hidden.astype(jnp.float32) + out_proj).astype(jnp.bfloat16)]
    unnamed x32 -> x17, local copies, waits for them, and re-layouts: 4.39 us -> 8.69 us
  transfers between devices with their start and end apart: 2 -> 0, of which waited for: 2 -> 0; matrix products, arithmetic and copies ran while one was open for 0% -> 0% of each run, Pallas kernels for 0% -> 0%
where the time goes in v1:
time: 145 us
  Pallas kernels  135 us (93%)
  local copies, waits for them, and re-layouts  9.39 us (6%)
    pallas_call x1, Pallas kernels, combine(): pl.pallas_call(combine_kernel, out_shape=jax.ShapeDtypeStruct((n_seq, n_n...  64.5 us
    pallas_call x1, Pallas kernels, attend(): pl.pallas_call(attend_kernel, grid=(n_seq, blocks), out_shape=jax.ShapeDt...  53.2 us
    pallas_call x1, Pallas kernels, project(): pl.pallas_call(project_kernel, out_shape=(jax.ShapeDtypeStruct((n_seq, 25...  17 us
    unnamed x17, local copies, waits for them, and re-layouts  8.69 us

profile of v1, /device:TPU:0, one launch (start us, length us, event | category | flops | bytes accessed | tf_op | source)
XLA Modules:
  0.0 144.8 jit_solution(14571920004248264335)
XLA Ops:
  0.6 0.7 broadcast_in_dim.9.an_ref
  1.3 0.0 copy-start
  1.3 1.3 copy-done
  2.6 0.0 copy-start.1
  2.6 1.3 copy-done.1
  4.0 0.0 copy-start.2
  4.0 0.7 copy-done.2
  4.6 0.0 copy-start.3
  4.6 0.7 copy-done.3
  5.3 0.0 copy-start.4
  5.3 0.7 copy-done.4
  5.9 0.0 copy-start.6
  5.9 0.7 copy-done.6
  6.6 0.0 copy-start.5
  6.6 17.0 %project.1 = (bf16[8,256,256]{2,1,0:T(8,128)(2,1)S(1)}, bf16[8,2,64,128]{3,2,1,0:T(8,128)(2,1)S(1)}, bf16[8,2,64,128]{3,2,1,0:T(8,128)(2,1)S(1)}) custom-call(s32[8]{0:T(128)S(1)} %copy-done.4, bf16[512,2560]{1,0:T(8,128)(2,1)} %bitcast.11, bf16[1,2560]{1,0:T(2,128)(2,1)S(1)} %broadcast_in_dim.9.an_ref, bf16[2560,1024]{1,0:T(8,128)(2,1)} %wq_hbm.1, ...), custom_call_target="tpu_custom_call" | custom-call | flops 4026531840 | bytes 12582912 | tf_op jit(solution)/shard_map/project/pallas_call | solution.py:78
  23.6 1.0 copy.16
  24.6 1.0 copy.15
  25.6 0.0 copy-done.5
  25.6 53.2 %attend.1.part_ref = f32[8,2,264,128]{3,2,1,0:T(8,128)S(1)} custom-call(s32[8]{0:T(128)S(1)} %copy-done.5, bf16[8,256,256]{2,1,0:T(8,128)(2,1)S(1)} %get-tuple-element.6.q_ref, bf16[8,8192,128]{2,1,0:T(8,128)(2,1)} %bitcast.12, bf16[8,8192,128]{2,1,0:T(8,128)(2,1)} %bitcast.13, bf16[8,2,64,128]{3,2,1,0:T(8,128)(2,1)S(1)} %get-tuple-element.7.k_own, ...), custom_call_target="tpu_custom_call" | custom-call | flops 18253611008 | bytes 37748736 | tf_op jit(solution)/shard_map/attend/pallas_call | solution.py:198
  78.8 64.5 %combine.1 = bf16[8,64,2560]{2,1,0:T(8,128)(2,1)S(1)} custom-call(f32[8,2,264,128]{3,2,1,0:T(8,128)S(1)} %attend.1.part_ref, bf16[8,64,2560]{2,1,0:T(8,128)(2,1)} %x_hbm.1, bf16[1024,2560]{1,0:T(8,128)(2,1)} %wo_hbm.1), custom_call_target="tpu_custom_call" | custom-call | flops 2147483648 | bytes 10485760 | tf_op jit(solution)/shard_map/combine/pallas_call | solution.py:410
  143.3 1.5 %copy.18 = bf16[8,64,2560]{2,1,0:T(8,128)(2,1)} copy(bf16[8,64,2560]{2,1,0:T(8,128)(2,1)S(1)} %combine.1) | data formatting | bytes 5242880
Async XLA Ops:
  1.3 1.3 copy-start
  2.6 1.3 copy-start.1
  4.0 0.7 copy-start.2
  4.6 0.7 copy-start.3
  5.3 0.7 copy-start.4
  5.9 0.7 copy-start.6
  6.6 19.0 %copy-start.5 = (s32[8]{0:T(128)S(1)}, s32[8]{0:T(128)}, u32[]{:S(2)}) copy-start(s32[8]{0:T(128)} %prefix_ref.3) | copy-start | bytes 100

commit v2 on v1

--- a/solution.py
+++ b/solution.py
@@ -17,6 +17,19 @@
 TN = (((0,), (0,)), ((), ()))
 F32 = jnp.float32
 BF16 = jnp.bfloat16
+VMEM_LIMIT = 67043328
+
+
+def cos_or_sin(x, want_cos):
+    quarter = jnp.floor(x * F32(2.0 / np.pi) + F32(0.5))
+    r = ((x - quarter * F32(1.5703125)) - quarter * F32(4.8351287841796875e-4)) - quarter * F32(3.13855707645416259765625e-7)
+    r = r - quarter * F32(6.077100628276710381e-11)
+    n = quarter.astype(jnp.int32) + want_cos.astype(jnp.int32)
+    r2 = r * r
+    sin_r = r + r * r2 * (F32(-1.6666654611e-1) + r2 * (F32(8.3321608736e-3) + r2 * F32(-1.9515295891e-4)))
+    cos_r = 1.0 - 0.5 * r2 + r2 * r2 * (F32(4.166664568298827e-2) + r2 * (F32(-1.388731625493765e-3) + r2 * F32(2.443315711809948e-5)))
+    y = jnp.where(n % 2 == 0, sin_r, cos_r)
+    return jnp.where(n % 4 >= 2, -y, y)
 
 
 def project_kernel(prefix_ref, x_ref, an_ref, wq_hbm, wk_hbm, wv_hbm, qn_ref, kn_ref, freq_ref,
@@ -32,13 +45,14 @@
         x = x_ref[r:r + 64, :].astype(F32)
         scale = lax.rsqrt(jnp.mean(x * x, axis=-1, keepdims=True) + EPS)
         normed[r:r + 64, :] = (x * scale * an_ref[...].astype(F32)).astype(BF16)
-    lane = lax.broadcasted_iota(jnp.int32, (n_new, HEAD_DIM), 1)
+    low = lax.broadcasted_iota(jnp.int32, (n_new, HEAD_DIM), 1) < HEAD_DIM // 2
     step = lax.broadcasted_iota(jnp.int32, (n_new, HEAD_DIM), 0)
     for b in range(n_seq):
         angle = (prefix_ref[b] + step).astype(F32) * freq_ref[...]
-        cos_ref[b * n_new:(b + 1) * n_new, :] = jnp.cos(angle)
-        sin_t = jnp.sin(angle)
-        sin_ref[b * n_new:(b + 1) * n_new, :] = jnp.where(lane < HEAD_DIM // 2, -sin_t, sin_t)
+        trig = cos_or_sin(angle, low)
+        turned = pltpu.roll(trig, HEAD_DIM // 2, 1)
+        cos_ref[b * n_new:(b + 1) * n_new, :] = jnp.where(low, trig, turned)
+        sin_ref[b * n_new:(b + 1) * n_new, :] = jnp.where(low, -turned, trig)
 
     def norm_rope(y, gain_ref):
         y = y.astype(BF16).astype(F32)
@@ -86,23 +100,30 @@
                         pltpu.VMEM((d_model, 256), BF16), pltpu.VMEM((rows, d_model), BF16),
                         pltpu.VMEM((rows, HEAD_DIM), F32), pltpu.VMEM((rows, HEAD_DIM), F32),
                         pltpu.SemaphoreType.DMA((6,))],
-        compiler_params=pltpu.CompilerParams(vmem_limit_bytes=48 << 20),
+        compiler_params=pltpu.CompilerParams(vmem_limit_bytes=VMEM_LIMIT),
         cost_estimate=pl.CostEstimate(flops=2 * rows * d_model * 1536, bytes_accessed=12 << 20, transcendentals=0),
         name="project",
     )(prefix_len, hidden.reshape(rows, d_model), attn_norm[None], w_q, w_k, w_v, q_norm[None], k_norm[None], freq)
 
 
+CHUNK = 2048
+SLOTS = 4
+
+
 def pair_reduce(op, x):
     x = op(x, pltpu.roll(x, 2, 0))
     return op(x, pltpu.roll(x, 4, 0))
 
 
-def own_keys(q, k_own_ref, v_own_ref, first):
+def split_heads(x, par_ref):
+    return jnp.concatenate([x * par_ref[h] for h in range(2)], axis=1)
+
+
+def own_keys(q, k_own_ref, v_own_ref):
     n_new = k_own_ref.shape[-2]
     key = lax.broadcasted_iota(jnp.int32, (n_new, 256), 0)
     col = lax.broadcasted_iota(jnp.int32, (n_new, 256), 1)
-    token = (col // 128) * 32 + col % 32
-    keep = jnp.logical_and(key <= token, first)
+    keep = key <= (col // 128) * 32 + col % 32
     maxes, sums, accs = [], [], []
     for h in range(2):
         s = lax.dot_general(k_own_ref[h], q[:, h * 128:(h + 1) * 128], NT, preferred_element_type=F32)
@@ -116,95 +137,156 @@
     return (jnp.where(even, maxes[0], maxes[1]), jnp.where(even, sums[0], sums[1]), accs)
 
 
-def block_scores(q, k_ref, s_ref, row0, limit, step=512):
-    rows = k_ref.shape[0]
-    even = (lax.broadcasted_iota(jnp.int32, (step, HEAD_DIM), 0) % 2 == 0)
-    even_f = even.astype(F32).astype(BF16)
-    odd_f = (1.0 - even.astype(F32)).astype(BF16)
-    row = lax.broadcasted_iota(jnp.int32, (step, 256), 0)
-    block_max = jnp.full((8, 256), MASKED, F32)
-    for r in range(0, rows, step):
-        k = k_ref[r:r + step, :]
-        both = jnp.concatenate([k * even_f, k * odd_f], axis=1)
-        s = lax.dot_general(both, q, NT, preferred_element_type=F32)
-        s = jnp.where(row < limit - (row0 + r), s, MASKED)
-        s_ref[r:r + step, :] = s
-        block_max = jnp.maximum(block_max, jnp.max(s.reshape(step // 8, 8, 256), axis=0))
-    return pair_reduce(jnp.maximum, block_max)
-
-
-def block_values(v_ref, s_ref, m8, step=1024):
-    rows = v_ref.shape[0]
-    even = (lax.broadcasted_iota(jnp.int32, (HEAD_DIM, step), 1) % 2 == 0)
-    even_f = even.astype(F32).astype(BF16)
-    odd_f = (1.0 - even.astype(F32)).astype(BF16)
-    l8 = jnp.zeros((8, 256), F32)
-    acc = None
-    for r in range(0, rows, step):
-        p = jnp.exp2(s_ref[r:r + step, :].reshape(step // 8, 8, 256) * LOG2_SCALE - m8[None])
-        l8 = l8 + jnp.sum(p, axis=0)
-        vt = v_ref[r:r + step, :].T
-        both = jnp.concatenate([vt * even_f, vt * odd_f], axis=0)
-        part = jnp.dot(both, p.reshape(step, 256).astype(BF16), preferred_element_type=F32)
-        acc = part if acc is None else acc + part
-    return pair_reduce(jnp.add, l8), acc
-
-
-def attend_kernel(prefix_ref, q_ref, k_ref, v_ref, k_own, v_own, o_ref, s_ref, m_ref, l_ref, acc_ref):
-    b, j = pl.program_id(0), pl.program_id(1)
-    rows = k_ref.shape[1]
+def attend_step(it, n_seq, per_seq, limit_of, q_all, k_ref, v_ref, k_own, v_own, par_ref, emit,
+                s_a, s_b, m_ref, l_ref, acc_ref, m_own, l_own, acc_own):
     cp = lax.axis_index("cp")
-    limit = 2 * prefix_ref[b] - cp * (rows * pl.num_programs(1))
-    q = q_ref[0]
-
-    @pl.when(j == 0)
+    s_refs = (s_a, s_b)
+
+    @pl.when(it == 0)
     def _():
-        m8, l8, accs = own_keys(q, k_own.at[0], v_own.at[0], cp == 0)
-        m_ref[...] = m8
-        l_ref[...] = l8
-        for h in range(2):
-            acc_ref[h * 128:(h + 1) * 128, :] = accs[h]
-
-    @pl.when(j * rows < limit)
+        even = (lax.broadcasted_iota(jnp.int32, (CHUNK, HEAD_DIM), 0) % 2 == 0).astype(F32)
+        par_ref[0] = even.astype(BF16)
+        par_ref[1] = (1.0 - even).astype(BF16)
+        acc_ref[...] = jnp.zeros_like(acc_ref)
+        l_ref[...] = jnp.zeros_like(l_ref)
+
+        @pl.when(cp == 0)
+        def _():
+            for b in range(n_seq):
+                m8, l8, accs = own_keys(q_all[b], k_own.at[b], v_own.at[b])
+                m_own[b] = m8
+                l_own[b] = l8
+                for h in range(2):
+                    acc_own[b, h * 128:(h + 1) * 128, :] = accs[h]
+
+        @pl.when(cp != 0)
+        def _():
+            m_own[...] = jnp.full_like(m_own, MASKED)
+            l_own[...] = jnp.zeros_like(l_own)
+            acc_own[...] = jnp.zeros_like(acc_own)
+
+    b_new, i = it // per_seq, it % per_seq
+    b_old = b_new - 1
+    rows = pl.ds(pl.multiple_of(i * CHUNK, CHUNK), CHUNK)
+
+    def score_dot():
+        both = split_heads(k_ref[...], par_ref)
+        return lax.dot_general(both, q_all[b_new], NT, preferred_element_type=F32)
+
+    def score_post(s, par):
+        keep = lax.broadcasted_iota(jnp.int32, (CHUNK, 128), 0) < limit_of(b_new) - i * CHUNK
+        s = jnp.concatenate([jnp.where(keep, s[:, 0:128], MASKED), jnp.where(keep, s[:, 128:256], MASKED)], axis=1)
+        s_refs[par][rows, :] = s
+        top = pair_reduce(jnp.maximum, jnp.max(s.reshape(CHUNK // 8, 8, 256), axis=0)) * LOG2_SCALE
+        m_ref[par] = jnp.maximum(jnp.where(i == 0, m_own[b_new], m_ref[par]), top)
+
+    def expo(par):
+        s = s_refs[par][rows, :]
+        p = jnp.exp2(s.reshape(CHUNK // 8, 8, 256) * LOG2_SCALE - m_ref[par][None])
+        l_ref[par] = jnp.where(i == 0, 0.0, l_ref[par]) + jnp.sum(p, axis=0)
+        return p.reshape(CHUNK, 256).astype(BF16)
+
+    def value(p):
+        both = split_heads(v_ref[...], par_ref)
+        part = lax.dot_general(both, p, TN, preferred_element_type=F32)
+        acc_ref[...] = jnp.where(i == 0, 0.0, acc_ref[...]) + part
+
+    total = n_seq * per_seq
+    scoring, adding = it < total, jnp.logical_and(it >= per_seq, it < total + per_seq)
+    for par in range(2):
+        @pl.when(b_new % 2 == par)
+        def _(par=par):
+            main = jnp.logical_and(scoring, adding)
+
+            @pl.when(main)
+            def _():
+                s = score_dot()
+                p = expo(1 - par)
+                value(p)
+                score_post(s, par)
+
+            @pl.when(jnp.logical_and(scoring, jnp.logical_not(adding)))
+            def _():
+                score_post(score_dot(), par)
+
+            @pl.when(jnp.logical_and(adding, jnp.logical_not(scoring)))
+            def _():
+                value(expo(1 - par))
+
+    @pl.when(jnp.logical_and(adding, i == per_seq - 1))
     def _():
-        block_max = block_scores(q, k_ref.at[0], s_ref, j * rows, limit)
-        m8 = jnp.maximum(m_ref[...], block_max * LOG2_SCALE)
-        alpha = jnp.exp2(m_ref[...] - m8)
-        l8, acc = block_values(v_ref.at[0], s_ref, m8)
-        m_ref[...] = m8
-        l_ref[...] = l_ref[...] * alpha + l8
-        for h in range(2):
-            part = slice(h * 128, (h + 1) * 128)
-            acc_ref[part, :] = acc_ref[part, :] * alpha[h:h + 1] + acc[part]
-
-    @pl.when(j == pl.num_programs(1) - 1)
-    def _():
+        b = b_old
+        m8 = m_ref[b % 2]
+        w = jnp.exp2(m_own[b] - m8)
+        l8 = pair_reduce(jnp.add, l_ref[b % 2]) + w * l_own[b]
         sub = lax.broadcasted_iota(jnp.int32, (8, 256), 0)
-        stats = jnp.where(sub < 2, m_ref[...], l_ref[...])
+        stats = jnp.where(sub < 2, m8, l8)
+        accs = [acc_ref[h * 128:(h + 1) * 128, :] + w[h:h + 1] * acc_own[b, h * 128:(h + 1) * 128, :] for h in range(2)]
+        emit(b, accs, stats)
+
+
+def attend_kernel(prefix_ref, q_ref, k_hbm, v_hbm, k_own, v_own, o_ref, par_ref, k_buf, v_buf, k_sem, v_sem, *scratch):
+    n_seq = q_ref.shape[0]
+    per_seq = pl.num_programs(0) // (n_seq + 1)
+    it = pl.program_id(0)
+    cp = lax.axis_index("cp")
+    fetch(it, n_seq * per_seq, per_seq, k_hbm, v_hbm, k_buf, v_buf, k_sem, v_sem)
+
+    def emit(b, accs, stats):
         for c in range(2):
-            o_ref[0, c, 0:256, :] = acc_ref[:, c * 128:(c + 1) * 128]
-            o_ref[0, c, 256:264, :] = stats[:, c * 128:(c + 1) * 128]
+            for h in range(2):
+                o_ref[b, c, h * 128:(h + 1) * 128, :] = accs[h][:, c * 128:(c + 1) * 128]
+            o_ref[b, c, 256:264, :] = stats[:, c * 128:(c + 1) * 128]
+
+    attend_step(it, n_seq, per_seq, lambda b: 2 * prefix_ref[b] - cp * (per_seq * CHUNK), q_ref, k_buf.at[it % SLOTS],
+                v_buf.at[it % SLOTS], k_own, v_own, par_ref, emit, *scratch)
+
+
+def fetch(it, total, per_seq, k_hbm, v_hbm, k_buf, v_buf, k_sem, v_sem):
+    def copy(hbm, buf, sem, lag, step):
+        j = step - lag
+        src = hbm.at[j // per_seq, pl.ds(pl.multiple_of((j % per_seq) * CHUNK, CHUNK), CHUNK), :]
+        return pltpu.make_async_copy(src, buf.at[step % SLOTS], sem.at[step % SLOTS])
+
+    for hbm, buf, sem, lag in ((k_hbm, k_buf, k_sem, 0), (v_hbm, v_buf, v_sem, per_seq)):
+        if lag == 0:
+            @pl.when(it == 0)
+            def _():
+                for step in range(SLOTS - 1):
+                    copy(hbm, buf, sem, lag, step).start()
+        ahead = it + SLOTS - 1
+
+        @pl.when(jnp.logical_and(ahead >= lag, ahead < total + lag))
+        def _():
+            copy(hbm, buf, sem, lag, ahead).start()
+
+        @pl.when(jnp.logical_and(it >= lag, it < total + lag))
+        def _():
+            copy(hbm, buf, sem, lag, it).wait()
 
 
 def attend(prefix_len, q, k_cache, v_cache, k_own, v_own):
     n_seq, slots = k_cache.shape[0], k_cache.shape[1]
-    rows = 4096
-    n_new = k_own.shape[2]
     k_rows = k_cache.reshape(n_seq, slots * 2, HEAD_DIM)
     v_rows = v_cache.reshape(n_seq, slots * 2, HEAD_DIM)
-    blocks = slots * 2 // rows
-    cache_spec = pl.BlockSpec((1, rows, HEAD_DIM), lambda b, j: (b, j, 0))
-    own_spec = pl.BlockSpec((1, 2, n_new, HEAD_DIM), lambda b, j: (b, 0, 0, 0))
+    per_seq = slots * 2 // CHUNK
+    total = n_seq * per_seq
+
+    vmem = pl.BlockSpec(memory_space=pltpu.VMEM)
     return pl.pallas_call(
         attend_kernel,
-        grid=(n_seq, blocks),
+        grid=(total + per_seq,),
         out_shape=jax.ShapeDtypeStruct((n_seq, 2, 264, 128), F32),
-        in_specs=[pl.BlockSpec(memory_space=pltpu.SMEM), pl.BlockSpec((1, 256, 256), lambda b, j: (b, 0, 0)),
-                  cache_spec, cache_spec, own_spec, own_spec],
-        out_specs=pl.BlockSpec((1, 2, 264, 128), lambda b, j: (b, 0, 0, 0)),
-        scratch_shapes=[pltpu.VMEM((rows, 256), F32), pltpu.VMEM((8, 256), F32), pltpu.VMEM((8, 256), F32),
-                        pltpu.VMEM((256, 256), F32)],
-        compiler_params=pltpu.CompilerParams(vmem_limit_bytes=40 << 20),
+        in_specs=[pl.BlockSpec(memory_space=pltpu.SMEM), vmem,
+                  pl.BlockSpec(memory_space=pl.ANY), pl.BlockSpec(memory_space=pl.ANY), vmem, vmem],
+        out_specs=vmem,
+        scratch_shapes=[pltpu.VMEM((2, CHUNK, HEAD_DIM), BF16), pltpu.VMEM((SLOTS, CHUNK, HEAD_DIM), BF16), pltpu.VMEM((SLOTS, CHUNK, HEAD_DIM), BF16),
+                        pltpu.SemaphoreType.DMA((SLOTS,)), pltpu.SemaphoreType.DMA((SLOTS,)),
+                        pltpu.VMEM((slots * 2, 256), F32), pltpu.VMEM((slots * 2, 256), F32),
+                        pltpu.VMEM((2, 8, 256), F32), pltpu.VMEM((2, 8, 256), F32), pltpu.VMEM((256, 256), F32),
+                        pltpu.VMEM((n_seq, 8, 256), F32), pltpu.VMEM((n_seq, 8, 256), F32),
+                        pltpu.VMEM((n_seq, 256, 256), F32)],
+        compiler_params=pltpu.CompilerParams(vmem_limit_bytes=VMEM_LIMIT),
         cost_estimate=pl.CostEstimate(flops=17 << 30, bytes_accessed=36 << 20, transcendentals=17 << 20),
         name="attend",
     )(prefix_len, q, k_rows, v_rows, k_own, v_own)
@@ -420,7 +502,7 @@
             pltpu.VMEM((units, 32, half), F32), pltpu.VMEM((4, units, 2, 32, half), F32),
             dma((1 + units,)), dma((n_seq,)), dma((n_seq,)), dma((units,)), dma((units,)), dma((units, 2)),
             dma((units, 2)), dma((units,)), dma((5, units, 2)), dma((4, units, 2))],
-        compiler_params=pltpu.CompilerParams(collective_id=0, has_side_effects=True, vmem_limit_bytes=48 << 20),
+        compiler_params=pltpu.CompilerParams(collective_id=0, has_side_effects=True, vmem_limit_bytes=VMEM_LIMIT),
         cost_estimate=pl.CostEstimate(flops=2 << 30, bytes_accessed=10 << 20, transcendentals=0),
         name="combine",
     )(parts, hidden, w_o)

time: 145 us -> 134 us (0.924)
  Pallas kernels: 135 us -> 125 us
    pallas_call x1, Pallas kernels: 53.2 us -> 40.1 us  [attend(): pl.pallas_call(attend_kernel, grid=(total + per_seq,), out_shape=jax.Shap...]
    pallas_call x1, Pallas kernels: 64.5 us -> 67.5 us  [combine(): pl.pallas_call(combine_kernel, out_shape=jax.ShapeDtypeStruct((n_seq, n_n...]
    unnamed x17 -> x3, local copies, waits for them, and re-layouts: 8.69 us -> 7.25 us
where the time goes in v2:
time: 134 us
  Pallas kernels  125 us (93%)
  local copies, waits for them, and re-layouts  8.54 us (6%)
    pallas_call x1, Pallas kernels, combine(): pl.pallas_call(combine_kernel, out_shape=jax.ShapeDtypeStruct((n_seq, n_n...  67.5 us
    pallas_call x1, Pallas kernels, attend(): pl.pallas_call(attend_kernel, grid=(total + per_seq,), out_shape=jax.Shap...  40.1 us
    pallas_call x1, Pallas kernels, project(): pl.pallas_call(project_kernel, out_shape=(jax.ShapeDtypeStruct((n_seq, 25...  17 us
    unnamed x3, local copies, waits for them, and re-layouts  7.25 us

profile of v2, /device:TPU:0, one launch (start us, length us, event | category | flops | bytes accessed | tf_op | source)
XLA Modules:
  0.0 133.8 jit_solution(1889214522764687173)
XLA Ops:
  0.6 1.3 broadcast_in_dim.9.an_ref
  1.9 17.0 %project.1 = (bf16[8,256,256]{2,1,0:T(8,128)(2,1)}, bf16[8,2,64,128]{3,2,1,0:T(8,128)(2,1)}, bf16[8,2,64,128]{3,2,1,0:T(8,128)(2,1)}) custom-call(s32[8]{0:T(128)} %prefix_ref.3, bf16[512,2560]{1,0:T(8,128)(2,1)} %bitcast.7, bf16[1,2560]{1,0:T(2,128)(2,1)} %broadcast_in_dim.9.an_ref, bf16[2560,1024]{1,0:T(8,128)(2,1)} %wq_hbm.1, bf16[2560,256]{1,0:T(8,128)(2,1)} %wk_hbm.1, ...), custom_call_target="tpu_custom_call" | custom-call | flops 4026531840 | bytes 12582912 | tf_op jit(solution)/shard_map/project/pallas_call | solution.py:92
  18.9 1.9 %copy.16 = bf16[8,64,2,128]{3,2,1,0:T(2,128)(2,1)} copy(bf16[8,64,2,128]{3,1,2,0:T(8,128)(2,1)} %bitcast.9) | data formatting | bytes 524288
  20.9 1.9 %copy.15 = bf16[8,64,2,128]{3,2,1,0:T(2,128)(2,1)} copy(bf16[8,64,2,128]{3,1,2,0:T(8,128)(2,1)} %bitcast.8) | data formatting | bytes 524288
  22.8 40.1 %attend.1.part_ref = f32[8,2,264,128]{3,2,1,0:T(8,128)} custom-call(s32[8]{0:T(128)} %prefix_ref.3, bf16[8,256,256]{2,1,0:T(8,128)(2,1)} %get-tuple-element.6.q_ref, bf16[8,8192,128]{2,1,0:T(8,128)(2,1)} %bitcast.10, bf16[8,8192,128]{2,1,0:T(8,128)(2,1)} %bitcast.11, bf16[8,2,64,128]{3,2,1,0:T(8,128)(2,1)} %get-tuple-element.7.k_own, ...), custom_call_target="tpu_custom_call" | custom-call | flops 18253611008 | bytes 37748736 | tf_op jit(solution)/shard_map/attend/pallas_call | solution.py:276
  62.9 67.5 %combine.1 = bf16[8,64,2560]{2,1,0:T(8,128)(2,1)} custom-call(f32[8,2,264,128]{3,2,1,0:T(8,128)} %attend.1.part_ref, bf16[8,64,2560]{2,1,0:T(8,128)(2,1)} %x_hbm.1, bf16[1024,2560]{1,0:T(8,128)(2,1)} %wo_hbm.1), custom_call_target="tpu_custom_call" | custom-call | flops 2147483648 | bytes 10485760 | tf_op jit(solution)/shard_map/combine/pallas_call | solution.py:492
  130.4 3.4 %copy.18 = bf16[8,64,2560]{2,1,0:T(8,128)(2,1)} copy(bf16[8,64,2560]{2,1,0:T(8,128)(2,1)} %combine.1) | data formatting | bytes 5242880

commit v3 on v2

--- a/solution.py
+++ b/solution.py
@@ -225,23 +225,6 @@
         emit(b, accs, stats)
 
 
-def attend_kernel(prefix_ref, q_ref, k_hbm, v_hbm, k_own, v_own, o_ref, par_ref, k_buf, v_buf, k_sem, v_sem, *scratch):
-    n_seq = q_ref.shape[0]
-    per_seq = pl.num_programs(0) // (n_seq + 1)
-    it = pl.program_id(0)
-    cp = lax.axis_index("cp")
-    fetch(it, n_seq * per_seq, per_seq, k_hbm, v_hbm, k_buf, v_buf, k_sem, v_sem)
-
-    def emit(b, accs, stats):
-        for c in range(2):
-            for h in range(2):
-                o_ref[b, c, h * 128:(h + 1) * 128, :] = accs[h][:, c * 128:(c + 1) * 128]
-            o_ref[b, c, 256:264, :] = stats[:, c * 128:(c + 1) * 128]
-
-    attend_step(it, n_seq, per_seq, lambda b: 2 * prefix_ref[b] - cp * (per_seq * CHUNK), q_ref, k_buf.at[it % SLOTS],
-                v_buf.at[it % SLOTS], k_own, v_own, par_ref, emit, *scratch)
-
-
 def fetch(it, total, per_seq, k_hbm, v_hbm, k_buf, v_buf, k_sem, v_sem):
     def copy(hbm, buf, sem, lag, step):
         j = step - lag
@@ -263,33 +246,6 @@
         @pl.when(jnp.logical_and(it >= lag, it < total + lag))
         def _():
             copy(hbm, buf, sem, lag, it).wait()
-
-
-def attend(prefix_len, q, k_cache, v_cache, k_own, v_own):
-    n_seq, slots = k_cache.shape[0], k_cache.shape[1]
-    k_rows = k_cache.reshape(n_seq, slots * 2, HEAD_DIM)
-    v_rows = v_cache.reshape(n_seq, slots * 2, HEAD_DIM)
-    per_seq = slots * 2 // CHUNK
-    total = n_seq * per_seq
-
-    vmem = pl.BlockSpec(memory_space=pltpu.VMEM)
-    return pl.pallas_call(
-        attend_kernel,
-        grid=(total + per_seq,),
-        out_shape=jax.ShapeDtypeStruct((n_seq, 2, 264, 128), F32),
-        in_specs=[pl.BlockSpec(memory_space=pltpu.SMEM), vmem,
-                  pl.BlockSpec(memory_space=pl.ANY), pl.BlockSpec(memory_space=pl.ANY), vmem, vmem],
-        out_specs=vmem,
-        scratch_shapes=[pltpu.VMEM((2, CHUNK, HEAD_DIM), BF16), pltpu.VMEM((SLOTS, CHUNK, HEAD_DIM), BF16), pltpu.VMEM((SLOTS, CHUNK, HEAD_DIM), BF16),
-                        pltpu.SemaphoreType.DMA((SLOTS,)), pltpu.SemaphoreType.DMA((SLOTS,)),
-                        pltpu.VMEM((slots * 2, 256), F32), pltpu.VMEM((slots * 2, 256), F32),
-                        pltpu.VMEM((2, 8, 256), F32), pltpu.VMEM((2, 8, 256), F32), pltpu.VMEM((256, 256), F32),
-                        pltpu.VMEM((n_seq, 8, 256), F32), pltpu.VMEM((n_seq, 8, 256), F32),
-                        pltpu.VMEM((n_seq, 256, 256), F32)],
-        compiler_params=pltpu.CompilerParams(vmem_limit_bytes=VMEM_LIMIT),
-        cost_estimate=pl.CostEstimate(flops=17 << 30, bytes_accessed=36 << 20, transcendentals=17 << 20),
-        name="attend",
-    )(prefix_len, q, k_rows, v_rows, k_own, v_own)
 
 
 def merge(parts):
@@ -304,9 +260,18 @@
     return accs, stats_out
 
 
-def combine_kernel(part_ref, x_hbm, wo_hbm, out_ref, x_buf, wo, ra1, sa2, ra2, proj, rs_o, rs_i, fwd, og,
-                   loc_sem, a1_s, a1_r, a2_s, a2_r, rs_s, rso_r, rsi_r, og_s, og_r):
-    n_seq = part_ref.shape[0]
+STAGES = 7
+LAGS = (3, 7, 12, 16, 20, 24, 28)
+
+
+def fused_kernel(prefix_ref, q_ref, k_hbm, v_hbm, k_own, v_own, x_hbm, wo_hbm, out_ref,
+                 par_ref, k_buf, v_buf, k_sem, v_sem, s_a, s_b, m_ref, l_ref, acc_ref, m_own, l_own, acc_own,
+                 part_ref, x_buf, wo, ra1, sa2, ra2, proj, rs_o, rs_i, fwd, og,
+                 loc_sem, a1_s, a1_r, a2_s, a2_r, rs_s, rso_r, rsi_r, og_s, og_r):
+    it = pl.program_id(0)
+    steps = pl.num_programs(0)
+    per_seq = steps // (q_ref.shape[0] + 1)
+    n_seq = q_ref.shape[0]
     units = n_seq // 2
     half_cols = proj.shape[-1]
     cp, z = lax.axis_index("cp"), lax.axis_index("tp")
@@ -326,26 +291,39 @@
                                             device_id=peer, device_id_type=MESH)
 
     wo_copy = pltpu.make_async_copy(wo_hbm, wo, loc_sem.at[0])
-    wo_copy.start()
     x_copies = [pltpu.make_async_copy(x_hbm.at[2 * u + y, pl.ds(32 * c, 32), :], x_buf.at[u], loc_sem.at[1 + u])
                 for u in range(units)]
-    for x_copy in x_copies:
-        x_copy.start()
-
-    barrier = pltpu.get_barrier_semaphore()
-    pl.semaphore_signal(barrier, inc=1, device_id=core_peer, device_id_type=MESH)
-    pl.semaphore_signal(barrier, inc=1, device_id=y_peer, device_id_type=MESH)
-
-    @pl.when(is_mid)
+
+    @pl.when(it == 0)
     def _():
-        pl.semaphore_signal(barrier, inc=1, device_id={"tp": outer}, device_id_type=MESH)
-        pl.semaphore_signal(barrier, inc=1, device_id={"tp": inner}, device_id_type=MESH)
-        pl.semaphore_wait(barrier, 4)
-
-    @pl.when(is_end)
+        barrier = pltpu.get_barrier_semaphore()
+        pl.semaphore_signal(barrier, inc=1, device_id=core_peer, device_id_type=MESH)
+        pl.semaphore_signal(barrier, inc=1, device_id=y_peer, device_id_type=MESH)
+
+        @pl.when(is_mid)
+        def _():
+            pl.semaphore_signal(barrier, inc=1, device_id={"tp": outer}, device_id_type=MESH)
+            pl.semaphore_signal(barrier, inc=1, device_id={"tp": inner}, device_id_type=MESH)
+            pl.semaphore_wait(barrier, 4)
+
+        @pl.when(is_end)
+        def _():
+            pl.semaphore_signal(barrier, inc=1, device_id={"tp": mid}, device_id_type=MESH)
+            pl.semaphore_wait(barrier, 3)
+
+    fetch(it, n_seq * per_seq, per_seq, k_hbm, v_hbm, k_buf, v_buf, k_sem, v_sem)
+
+    @pl.when(it == 1)
     def _():
-        pl.semaphore_signal(barrier, inc=1, device_id={"tp": mid}, device_id_type=MESH)
-        pl.semaphore_wait(barrier, 3)
+        wo_copy.start()
+        for x_copy in x_copies:
+            x_copy.start()
+
+    @pl.when(it == 2 * per_seq)
+    def _():
+        wo_copy.wait()
+        for x_copy in x_copies:
+            x_copy.wait()
 
     def a1(b):
         return remote(part_ref.at[b, 1 - c], ra1.at[b], a1_s.at[b], a1_r.at[b], core_peer)
@@ -362,8 +340,16 @@
     def gather(q, u, half, lane, peer):
         return remote(og.at[q, u, half], og.at[q, u, half], og_s.at[lane, u, half], og_r.at[q, u, half], peer)
 
-    for b in range(n_seq):
+    def emit(b, accs, stats):
+        for core in range(2):
+            for h in range(2):
+                part_ref[b, core, h * 128:(h + 1) * 128, :] = accs[h][:, core * 128:(core + 1) * 128]
+            part_ref[b, core, 256:264, :] = stats[:, core * 128:(core + 1) * 128]
         a1(b).start()
+
+    attend_step(it, n_seq, per_seq, lambda b: 2 * prefix_ref[b] - cp * (per_seq * CHUNK), q_ref, k_buf.at[it % SLOTS],
+                v_buf.at[it % SLOTS], k_own, v_own, par_ref, emit,
+                s_a, s_b, m_ref, l_ref, acc_ref, m_own, l_own, acc_own)
 
     def s1(u):
         b = 2 * u + 1 - y
@@ -445,56 +431,68 @@
                 out_ref[2 * u + q // 2, 32 * (q % 2):32 * (q % 2) + 32, half * half_cols:(half + 1) * half_cols] = (
                     og[q, u, half].astype(BF16))
 
-    wo_copy.wait()
-    for x_copy in x_copies:
-        x_copy.wait()
     stages = (s1, s2, s3, s4, s5, s6, s7)
 
     def slot(t, carry):
-        for i, stage in enumerate(stages):
-            @pl.when(jnp.logical_and(t >= i, t < units + i))
-            def _(stage=stage, i=i):
-                stage(t - i)
+        for stage, lag in zip(stages, LAGS):
+            since = t - (3 * per_seq - 1) - lag
+            @pl.when(jnp.logical_and(since >= 0, jnp.logical_and(since < 2 * per_seq * units, since % (2 * per_seq) == 0)))
+            def _(stage=stage, since=since):
+                stage(since // (2 * per_seq))
         return carry
 
-    lax.fori_loop(0, units + len(stages) - 1, slot, 0)
-
-    for b in range(n_seq):
-        a1(b).wait_send()
-    for u in range(units):
-        a2(u).wait_send()
-        for half in (near, far):
-            gather(me, u, half, 0, core_peer).wait_send()
-            gather(me, u, half, 1, y_peer).wait_send()
-            gather(yq, u, half, 4, core_peer).wait_send()
-
-    @pl.when(is_end)
+    last = (2 * units + 1) * per_seq - 1 + LAGS[-1]
+    lax.fori_loop(it, jnp.where(it == steps - 1, last + 1, it + 1), slot, 0)
+
+    @pl.when(it == steps - 1)
     def _():
+        for b in range(n_seq):
+            a1(b).wait_send()
         for u in range(units):
+            a2(u).wait_send()
             for half in (near, far):
-                rs_out(u, half).wait_send()
-
-    @pl.when(is_mid)
-    def _():
-        for u in range(units):
-            rs_in(u).wait_send()
-            gather(me, u, near, 2, {"tp": inner}).wait_send()
-            for half in (near, far):
-                gather(me, u, half, 3, {"tp": outer}).wait_send()
-
-
-def combine(parts, hidden, w_o):
+                gather(me, u, half, 0, core_peer).wait_send()
+                gather(me, u, half, 1, y_peer).wait_send()
+                gather(yq, u, half, 4, core_peer).wait_send()
+
+        @pl.when(is_end)
+        def _():
+            for u in range(units):
+                for half in (near, far):
+                    rs_out(u, half).wait_send()
+
+        @pl.when(is_mid)
+        def _():
+            for u in range(units):
+                rs_in(u).wait_send()
+                gather(me, u, near, 2, {"tp": inner}).wait_send()
+                for half in (near, far):
+                    gather(me, u, half, 3, {"tp": outer}).wait_send()
+
+
+def attend_and_combine(prefix_len, q, k_cache, v_cache, k_own, v_own, hidden, w_o):
     n_seq, n_new, d_model = hidden.shape
+    slots = k_cache.shape[1]
+    k_rows = k_cache.reshape(n_seq, slots * 2, HEAD_DIM)
+    v_rows = v_cache.reshape(n_seq, slots * 2, HEAD_DIM)
+    per_seq = slots * 2 // CHUNK
     units, half = n_seq // 2, d_model // 2
     vmem = pl.BlockSpec(memory_space=pltpu.VMEM)
     hbm = pl.BlockSpec(memory_space=pl.ANY)
     dma = pltpu.SemaphoreType.DMA
     return pl.pallas_call(
-        combine_kernel,
+        fused_kernel,
+        grid=((n_seq + 1) * per_seq,),
         out_shape=jax.ShapeDtypeStruct((n_seq, n_new, d_model), BF16),
-        in_specs=[vmem, hbm, hbm],
+        in_specs=[pl.BlockSpec(memory_space=pltpu.SMEM), vmem, hbm, hbm, vmem, vmem, hbm, hbm],
         out_specs=vmem,
         scratch_shapes=[
+            pltpu.VMEM((2, CHUNK, HEAD_DIM), BF16), pltpu.VMEM((SLOTS, CHUNK, HEAD_DIM), BF16),
+            pltpu.VMEM((SLOTS, CHUNK, HEAD_DIM), BF16), dma((SLOTS,)), dma((SLOTS,)),
+            pltpu.VMEM((slots * 2, 256), F32), pltpu.VMEM((slots * 2, 256), F32),
+            pltpu.VMEM((2, 8, 256), F32), pltpu.VMEM((2, 8, 256), F32), pltpu.VMEM((256, 256), F32),
+            pltpu.VMEM((n_seq, 8, 256), F32), pltpu.VMEM((n_seq, 8, 256), F32), pltpu.VMEM((n_seq, 256, 256), F32),
+            pltpu.VMEM((n_seq, 2, 264, 128), F32),
             pltpu.VMEM((units, 32, d_model), BF16), pltpu.VMEM(w_o.shape, BF16),
             pltpu.VMEM((n_seq, 264, 128), F32), pltpu.VMEM((units, 264, 128), F32),
             pltpu.VMEM((units, 264, 128), F32), pltpu.VMEM((units, 2, 32, half), F32),
@@ -502,17 +500,16 @@
             pltpu.VMEM((units, 32, half), F32), pltpu.VMEM((4, units, 2, 32, half), F32),
             dma((1 + units,)), dma((n_seq,)), dma((n_seq,)), dma((units,)), dma((units,)), dma((units, 2)),
             dma((units, 2)), dma((units,)), dma((5, units, 2)), dma((4, units, 2))],
-        compiler_params=pltpu.CompilerParams(collective_id=0, has_side_effects=True, vmem_limit_bytes=VMEM_LIMIT),
-        cost_estimate=pl.CostEstimate(flops=2 << 30, bytes_accessed=10 << 20, transcendentals=0),
-        name="combine",
-    )(parts, hidden, w_o)
+        compiler_params=pltpu.CompilerParams(collective_id=0, has_side_effects=True, vmem_limit_bytes=56 << 20),
+        cost_estimate=pl.CostEstimate(flops=19 << 30, bytes_accessed=46 << 20, transcendentals=17 << 20),
+        name="attend_and_combine",
+    )(prefix_len, q, k_rows, v_rows, k_own, v_own, hidden, w_o)
 
 
 def solution(mesh):
     def per_device(hidden, prefix_len, k_cache, v_cache, attn_norm, w_q, w_k, w_v, w_o, q_norm, k_norm):
         q, k_own, v_own = project(hidden, prefix_len, attn_norm, w_q, w_k, w_v, q_norm, k_norm)
-        parts = attend(prefix_len, q, k_cache, v_cache, k_own, v_own)
-        block_out = combine(parts, hidden, w_o)
+        block_out = attend_and_combine(prefix_len, q, k_cache, v_cache, k_own, v_own, hidden, w_o)
         return block_out, k_own.transpose(0, 2, 1, 3), v_own.transpose(0, 2, 1, 3)
 
     cache_spec = P('dp', 'cp', 'tp', None)

time: 134 us -> 124 us (0.925)
  Pallas kernels: 125 us -> 115 us
    pallas_call x2 -> x1, Pallas kernels: 108 us -> 97.6 us  [attend_and_combine(): pl.pallas_call(fused_kernel, grid=((n_seq + 1) * per_seq,), out_shape=jax...]
where the time goes in v3:
time: 124 us
  Pallas kernels  115 us (93%)
  local copies, waits for them, and re-layouts  8.54 us (7%)
    pallas_call x1, Pallas kernels, attend_and_combine(): pl.pallas_call(fused_kernel, grid=((n_seq + 1) * per_seq,), out_shape=jax...  97.6 us
    pallas_call x1, Pallas kernels, project(): pl.pallas_call(project_kernel, out_shape=(jax.ShapeDtypeStruct((n_seq, 25...  17 us
    unnamed x3, local copies, waits for them, and re-layouts  7.25 us

profile of v3, /device:TPU:0, one launch (start us, length us, event | category | flops | bytes accessed | tf_op | source)
XLA Modules:
  0.0 123.8 jit_solution(35382853974370836)
XLA Ops:
  0.6 1.3 %broadcast_in_dim.9.an_ref = bf16[1,2560]{1,0:T(2,128)(2,1)} reshape(bf16[2560]{0:T(1024)(128)(2,1)} %param.16) | data formatting | bytes 10240 | tf_op jit(solution)/shard_map/broadcast_in_dim | solution.py:106
  1.9 17.0 %project.1 = (bf16[8,256,256]{2,1,0:T(8,128)(2,1)}, bf16[8,2,64,128]{3,2,1,0:T(8,128)(2,1)}, bf16[8,2,64,128]{3,2,1,0:T(8,128)(2,1)}) custom-call(s32[8]{0:T(128)} %prefix_ref.3, bf16[512,2560]{1,0:T(8,128)(2,1)} %bitcast.11, bf16[1,2560]{1,0:T(2,128)(2,1)} %broadcast_in_dim.9.an_ref, bf16[2560,1024]{1,0:T(8,128)(2,1)} %wq_hbm.1, bf16[2560,256]{1,0:T(8,128)(2,1)} %wk_hbm.1, ...), custom_call_target="tpu_custom_call" | custom-call | flops 4026531840 | bytes 12582912 | tf_op jit(solution)/shard_map/project/pallas_call | solution.py:92
  18.9 1.9 %copy.16 = bf16[8,64,2,128]{3,2,1,0:T(2,128)(2,1)} copy(bf16[8,64,2,128]{3,1,2,0:T(8,128)(2,1)} %bitcast.8) | data formatting | bytes 524288
  20.9 1.9 %copy.15 = bf16[8,64,2,128]{3,2,1,0:T(2,128)(2,1)} copy(bf16[8,64,2,128]{3,1,2,0:T(8,128)(2,1)} %bitcast.7) | data formatting | bytes 524288
  22.8 97.6 %attend_and_combine.1 = bf16[8,64,2560]{2,1,0:T(8,128)(2,1)} custom-call(s32[8]{0:T(128)} %prefix_ref.3, bf16[8,256,256]{2,1,0:T(8,128)(2,1)} %get-tuple-element.6.q_ref, bf16[8,8192,128]{2,1,0:T(8,128)(2,1)} %bitcast.9, bf16[8,8192,128]{2,1,0:T(8,128)(2,1)} %bitcast.10, bf16[8,2,64,128]{3,2,1,0:T(8,128)(2,1)} %get-tuple-element.7.k_own, ...), custom_call_target="tpu_custom_call" | custom-call | flops 20401094656 | bytes 48234496 | tf_op jit(solution)/shard_map/attend_and_combine/pallas_call | solution.py:483
  120.4 3.4 %copy.18 = bf16[8,64,2560]{2,1,0:T(8,128)(2,1)} copy(bf16[8,64,2560]{2,1,0:T(8,128)(2,1)} %attend_and_combine.1) | data formatting | bytes 5242880

commit v4 on v3

--- a/solution.py
+++ b/solution.py
@@ -33,7 +33,7 @@
 
 
 def project_kernel(prefix_ref, x_ref, an_ref, wq_hbm, wk_hbm, wv_hbm, qn_ref, kn_ref, freq_ref,
-                   q_ref, k_ref, v_ref, wq, wk, wv, normed, cos_ref, sin_ref, sems):
+                   q_ref, k_ref, v_ref, kn_out, vn_out, wq, wk, wv, normed, cos_ref, sin_ref, sems):
     n_seq, n_new = k_ref.shape[0], k_ref.shape[2]
     rows = n_seq * n_new
     copies = [pltpu.make_async_copy(wq_hbm.at[:, pl.ds(256 * j, 256)], wq.at[j], sems.at[j]) for j in range(4)]
@@ -69,17 +69,23 @@
                 for c in range(2):
                     q_ref[b, c * 128 + g * 32:c * 128 + g * 32 + 32, h * 128:(h + 1) * 128] = (
                         head[b * 64 + c * 32:b * 64 + c * 32 + 32])
+    dst = lax.broadcasted_iota(jnp.int32, (2 * n_new, 2 * n_new), 0)
+    src = lax.broadcasted_iota(jnp.int32, (2 * n_new, 2 * n_new), 1)
+    perm = (src == (dst % 2) * n_new + dst // 2).astype(F32).astype(BF16)
+
+    def put(heads, own_ref, new_ref):
+        for b in range(n_seq):
+            both = jnp.concatenate([head[b * n_new:(b + 1) * n_new] for head in heads], axis=0)
+            for h in range(2):
+                own_ref[b, h] = both[h * n_new:(h + 1) * n_new]
+            new_ref[b] = jnp.dot(perm, both, preferred_element_type=F32).astype(BF16)
+
     copies[4].wait()
     y = jnp.dot(normed[...], wk[...], preferred_element_type=F32)
-    for h in range(2):
-        head = norm_rope(y[:, h * HEAD_DIM:(h + 1) * HEAD_DIM], kn_ref)
-        for b in range(n_seq):
-            k_ref[b, h] = head[b * 64:(b + 1) * 64]
+    put([norm_rope(y[:, h * HEAD_DIM:(h + 1) * HEAD_DIM], kn_ref) for h in range(2)], k_ref, kn_out)
     copies[5].wait()
     y = jnp.dot(normed[...], wv[...], preferred_element_type=F32).astype(BF16)
-    for h in range(2):
-        for b in range(n_seq):
-            v_ref[b, h] = y[b * 64:(b + 1) * 64, h * HEAD_DIM:(h + 1) * HEAD_DIM]
+    put([y[:, h * HEAD_DIM:(h + 1) * HEAD_DIM] for h in range(2)], v_ref, vn_out)
 
 
 def project(hidden, prefix_len, attn_norm, w_q, w_k, w_v, q_norm, k_norm):
@@ -93,9 +99,11 @@
         project_kernel,
         out_shape=(jax.ShapeDtypeStruct((n_seq, 256, 256), BF16),
                    jax.ShapeDtypeStruct((n_seq, 2, n_new, HEAD_DIM), BF16),
-                   jax.ShapeDtypeStruct((n_seq, 2, n_new, HEAD_DIM), BF16)),
+                   jax.ShapeDtypeStruct((n_seq, 2, n_new, HEAD_DIM), BF16),
+                   jax.ShapeDtypeStruct((n_seq, 2 * n_new, HEAD_DIM), BF16),
+                   jax.ShapeDtypeStruct((n_seq, 2 * n_new, HEAD_DIM), BF16)),
         in_specs=[pl.BlockSpec(memory_space=pltpu.SMEM), vmem, vmem, hbm, hbm, hbm, vmem, vmem, vmem],
-        out_specs=(vmem, vmem, vmem),
+        out_specs=(vmem,) * 5,
         scratch_shapes=[pltpu.VMEM((4, d_model, 256), BF16), pltpu.VMEM((d_model, 256), BF16),
                         pltpu.VMEM((d_model, 256), BF16), pltpu.VMEM((rows, d_model), BF16),
                         pltpu.VMEM((rows, HEAD_DIM), F32), pltpu.VMEM((rows, HEAD_DIM), F32),
@@ -174,7 +182,8 @@
         return lax.dot_general(both, q_all[b_new], NT, preferred_element_type=F32)
 
     def score_post(s, par):
-        keep = lax.broadcasted_iota(jnp.int32, (CHUNK, 128), 0) < limit_of(b_new) - i * CHUNK
+        left = limit_of(b_new) - i * CHUNK - lax.broadcasted_iota(jnp.int32, (8, 128), 0)
+        keep = (lax.broadcasted_iota(jnp.int32, (CHUNK // 8, 8, 128), 0) * 8 < left[None]).reshape(CHUNK, 128)
         s = jnp.concatenate([jnp.where(keep, s[:, 0:128], MASKED), jnp.where(keep, s[:, 128:256], MASKED)], axis=1)
         s_refs[par][rows, :] = s
         top = pair_reduce(jnp.maximum, jnp.max(s.reshape(CHUNK // 8, 8, 256), axis=0)) * LOG2_SCALE
@@ -261,7 +270,8 @@
 
 
 STAGES = 7
-LAGS = (3, 7, 12, 16, 20, 24, 28)
+PIECES = 5
+LAGS = (3, 7, 11, 15, 18, 22, 24)
 
 
 def fused_kernel(prefix_ref, q_ref, k_hbm, v_hbm, k_own, v_own, x_hbm, wo_hbm, out_ref,
@@ -273,7 +283,7 @@
     per_seq = steps // (q_ref.shape[0] + 1)
     n_seq = q_ref.shape[0]
     units = n_seq // 2
-    half_cols = proj.shape[-1]
+    pieces, width = proj.shape[2], proj.shape[-1]
     cp, z = lax.axis_index("cp"), lax.axis_index("tp")
     y, c = cp // 2, cp % 2
     is_mid = jnp.logical_and(z >= 1, z <= 2)
@@ -331,14 +341,14 @@
     def a2(u):
         return remote(sa2.at[u], ra2.at[u], a2_s.at[u], a2_r.at[u], y_peer)
 
-    def rs_out(u, half):
-        return remote(proj.at[u, half], rs_o.at[u, half], rs_s.at[u, half], rso_r.at[u, half], {"tp": mid})
-
-    def rs_in(u):
-        return remote(fwd.at[u], rs_i.at[u], rs_s.at[u, 0], rsi_r.at[u], {"tp": inner})
-
-    def gather(q, u, half, lane, peer):
-        return remote(og.at[q, u, half], og.at[q, u, half], og_s.at[lane, u, half], og_r.at[q, u, half], peer)
+    def rs_out(u, half, p):
+        return remote(proj.at[u, half, p], rs_o.at[u, half, p], rs_s.at[u, half, p], rso_r.at[u, half, p], {"tp": mid})
+
+    def rs_in(u, p):
+        return remote(fwd.at[u, p], rs_i.at[u, p], rs_s.at[u, 0, p], rsi_r.at[u, p], {"tp": inner})
+
+    def gather(q, u, half, p, lane, peer):
+        return remote(og.at[q, u, half, p], og.at[q, u, half, p], og_s.at[lane, u, half, p], og_r.at[q, u, half, p], peer)
 
     def emit(b, accs, stats):
         for core in range(2):
@@ -370,66 +380,73 @@
             o = (accs[h] / stats[2 + h:3 + h]).T.astype(BF16)
             heads += [o[g * 32:(g + 1) * 32] for g in range(4)]
         o = jnp.concatenate(heads, axis=1)
-        for half in range(2):
-            proj[u, half] = jnp.dot(o, wo[:, half * half_cols:(half + 1) * half_cols], preferred_element_type=F32)
-
-        @pl.when(is_end)
-        def _():
-            rs_out(u, far).start()
-            rs_out(u, near).start()
+        for half in (far, near):
+            for p in range(pieces):
+                cols = pl.ds(pl.multiple_of((half * pieces + p) * width, width), width)
+                proj[u, half, p] = jnp.dot(o, wo[:, cols], preferred_element_type=F32)
+
+                @pl.when(is_end)
+                def _(half=half, p=p):
+                    rs_out(u, half, p).start()
 
     def s3(u):
         @pl.when(is_mid)
         def _():
-            rs_out(u, far).wait_recv()
-            fwd[u] = proj[u, far] + rs_o[u, far]
-            rs_in(u).start()
-
-    def x_half(u):
-        lo = x_buf[u, :, 0:half_cols].astype(F32)
-        hi = x_buf[u, :, half_cols:2 * half_cols].astype(F32)
-        return jnp.where(near == 0, lo, hi)
+            for p in range(pieces):
+                rs_out(u, far, p).wait_recv()
+                fwd[u, p] = proj[u, far, p] + rs_o[u, far, p]
+                rs_in(u, p).start()
 
     def s4(u):
-        @pl.when(is_mid)
-        def _():
-            rs_out(u, near).wait_recv()
-            rs_in(u).wait_recv()
-            total = (proj[u, near] + rs_o[u, near]) + rs_i[u]
-            og[me, u, near] = (x_half(u) + total).astype(BF16).astype(F32)
-            gather(me, u, near, 2, {"tp": inner}).start()
-            gather(me, u, near, 3, {"tp": outer}).start()
-
-        @pl.when(is_end)
-        def _():
-            gather(me, u, near, 2, {"tp": mid}).wait_recv()
-
-        gather(me, u, near, 1, y_peer).start()
-        gather(me, u, near, 0, core_peer).start()
+        for p in range(pieces):
+            @pl.when(is_mid)
+            def _(p=p):
+                rs_out(u, near, p).wait_recv()
+                rs_in(u, p).wait_recv()
+                total = (proj[u, near, p] + rs_o[u, near, p]) + rs_i[u, p]
+                x = x_buf[u, :, pl.ds(pl.multiple_of((near * pieces + p) * width, width), width)].astype(F32)
+                og[me, u, near, p] = (x + total).astype(BF16).astype(F32)
+                gather(me, u, near, p, 2, {"tp": inner}).start()
+                gather(me, u, near, p, 3, {"tp": outer}).start()
+
+            @pl.when(is_end)
+            def _(p=p):
+                gather(me, u, near, p, 2, {"tp": mid}).wait_recv()
+
+            gather(me, u, near, p, 1, y_peer).start()
+            gather(me, u, near, p, 0, core_peer).start()
 
     def s5(u):
-        gather(me, u, far, 2, {"tp": inner}).wait_recv()
-
-        @pl.when(is_mid)
-        def _():
-            gather(me, u, far, 3, {"tp": outer}).start()
-
-        gather(me, u, far, 1, y_peer).start()
-        gather(me, u, far, 0, core_peer).start()
+        for p in range(pieces):
+            gather(me, u, far, p, 2, {"tp": inner}).wait_recv()
+
+            @pl.when(is_mid)
+            def _(p=p):
+                gather(me, u, far, p, 3, {"tp": outer}).start()
+
+            gather(me, u, far, p, 1, y_peer).start()
+            gather(me, u, far, p, 0, core_peer).start()
 
     def s6(u):
         for half in (near, far):
-            gather(yq, u, half, 1, y_peer).wait_recv()
-            gather(yq, u, half, 4, core_peer).start()
+            for p in range(pieces):
+                gather(yq, u, half, p, 1, y_peer).wait_recv()
+                gather(yq, u, half, p, 4, core_peer).start()
+
+    def put(q, u, half, p):
+        cols = pl.ds(pl.multiple_of((half * pieces + p) * width, width), width)
+        out_ref[2 * u + q // 2, pl.ds(pl.multiple_of(32 * (q % 2), 32), 32), cols] = og[q, u, half, p].astype(BF16)
 
     def s7(u):
+        for half in (near, far):
+            for p in range(pieces):
+                put(me, u, half, p)
+                put(yq, u, half, p)
         for q in (y * 2 + 1 - c, (1 - y) * 2 + 1 - c):
-            for half in range(2):
-                gather(q, u, half, 0, core_peer).wait_recv()
-        for q in range(4):
-            for half in range(2):
-                out_ref[2 * u + q // 2, 32 * (q % 2):32 * (q % 2) + 32, half * half_cols:(half + 1) * half_cols] = (
-                    og[q, u, half].astype(BF16))
+            for half in (near, far):
+                for p in range(pieces):
+                    gather(q, u, half, p, 0, core_peer).wait_recv()
+                    put(q, u, half, p)
 
     stages = (s1, s2, s3, s4, s5, s6, s7)
 
@@ -451,23 +468,26 @@
         for u in range(units):
             a2(u).wait_send()
             for half in (near, far):
-                gather(me, u, half, 0, core_peer).wait_send()
-                gather(me, u, half, 1, y_peer).wait_send()
-                gather(yq, u, half, 4, core_peer).wait_send()
+                for p in range(pieces):
+                    gather(me, u, half, p, 0, core_peer).wait_send()
+                    gather(me, u, half, p, 1, y_peer).wait_send()
+                    gather(yq, u, half, p, 4, core_peer).wait_send()
 
         @pl.when(is_end)
         def _():
             for u in range(units):
                 for half in (near, far):
-                    rs_out(u, half).wait_send()
+                    for p in range(pieces):
+                        rs_out(u, half, p).wait_send()
 
         @pl.when(is_mid)
         def _():
             for u in range(units):
-                rs_in(u).wait_send()
-                gather(me, u, near, 2, {"tp": inner}).wait_send()
-                for half in (near, far):
-                    gather(me, u, half, 3, {"tp": outer}).wait_send()
+                for p in range(pieces):
+                    rs_in(u, p).wait_send()
+                    gather(me, u, near, p, 2, {"tp": inner}).wait_send()
+                    for half in (near, far):
+                        gather(me, u, half, p, 3, {"tp": outer}).wait_send()
 
 
 def attend_and_combine(prefix_len, q, k_cache, v_cache, k_own, v_own, hidden, w_o):
@@ -476,7 +496,7 @@
     k_rows = k_cache.reshape(n_seq, slots * 2, HEAD_DIM)
     v_rows = v_cache.reshape(n_seq, slots * 2, HEAD_DIM)
     per_seq = slots * 2 // CHUNK
-    units, half = n_seq // 2, d_model // 2
+    units, width = n_seq // 2, d_model // (2 * PIECES)
     vmem = pl.BlockSpec(memory_space=pltpu.VMEM)
     hbm = pl.BlockSpec(memory_space=pl.ANY)
     dma = pltpu.SemaphoreType.DMA
@@ -495,11 +515,11 @@
             pltpu.VMEM((n_seq, 2, 264, 128), F32),
             pltpu.VMEM((units, 32, d_model), BF16), pltpu.VMEM(w_o.shape, BF16),
             pltpu.VMEM((n_seq, 264, 128), F32), pltpu.VMEM((units, 264, 128), F32),
-            pltpu.VMEM((units, 264, 128), F32), pltpu.VMEM((units, 2, 32, half), F32),
-            pltpu.VMEM((units, 2, 32, half), F32), pltpu.VMEM((units, 32, half), F32),
-            pltpu.VMEM((units, 32, half), F32), pltpu.VMEM((4, units, 2, 32, half), F32),
-            dma((1 + units,)), dma((n_seq,)), dma((n_seq,)), dma((units,)), dma((units,)), dma((units, 2)),
-            dma((units, 2)), dma((units,)), dma((5, units, 2)), dma((4, units, 2))],
+            pltpu.VMEM((units, 264, 128), F32), pltpu.VMEM((units, 2, PIECES, 32, width), F32),
+            pltpu.VMEM((units, 2, PIECES, 32, width), F32), pltpu.VMEM((units, PIECES, 32, width), F32),
+            pltpu.VMEM((units, PIECES, 32, width), F32), pltpu.VMEM((4, units, 2, PIECES, 32, width), F32),
+            dma((1 + units,)), dma((n_seq,)), dma((n_seq,)), dma((units,)), dma((units,)), dma((units, 2, PIECES)),
+            dma((units, 2, PIECES)), dma((units, PIECES)), dma((5, units, 2, PIECES)), dma((4, units, 2, PIECES))],
         compiler_params=pltpu.CompilerParams(collective_id=0, has_side_effects=True, vmem_limit_bytes=56 << 20),
         cost_estimate=pl.CostEstimate(flops=19 << 30, bytes_accessed=46 << 20, transcendentals=17 << 20),
         name="attend_and_combine",
@@ -508,9 +528,10 @@
 
 def solution(mesh):
     def per_device(hidden, prefix_len, k_cache, v_cache, attn_norm, w_q, w_k, w_v, w_o, q_norm, k_norm):
-        q, k_own, v_own = project(hidden, prefix_len, attn_norm, w_q, w_k, w_v, q_norm, k_norm)
+        q, k_own, v_own, k_new, v_new = project(hidden, prefix_len, attn_norm, w_q, w_k, w_v, q_norm, k_norm)
         block_out = attend_and_combine(prefix_len, q, k_cache, v_cache, k_own, v_own, hidden, w_o)
-        return block_out, k_own.transpose(0, 2, 1, 3), v_own.transpose(0, 2, 1, 3)
+        shape = (hidden.shape[0], hidden.shape[1], 2, HEAD_DIM)
+        return block_out, k_new.reshape(shape), v_new.reshape(shape)
 
     cache_spec = P('dp', 'cp', 'tp', None)
     arg_specs = (P('dp', None, None), P('dp'), cache_spec, cache_spec, P(None), P(None, 'tp'), P(None, 'tp'), P(None, 'tp'), P('tp', None), P(None), P(None))

time: 124 us -> 119 us (0.960)
  local copies, waits for them, and re-layouts: 8.54 us -> 4.69 us
    unnamed x3 -> x1, local copies, waits for them, and re-layouts: 7.25 us -> 3.4 us
where the time goes in v4:
time: 119 us
  Pallas kernels  114 us (96%)
  local copies, waits for them, and re-layouts  4.69 us (4%)
    pallas_call x1, Pallas kernels, attend_and_combine(): pl.pallas_call(fused_kernel, grid=((n_seq + 1) * per_seq,), out_shape=jax...  96.4 us
    pallas_call x1, Pallas kernels, project(): pl.pallas_call(project_kernel, out_shape=(jax.ShapeDtypeStruct((n_seq, 25...  17.3 us
    unnamed x1, local copies, waits for them, and re-layouts  3.4 us

profile of v4, /device:TPU:0, one launch (start us, length us, event | category | flops | bytes accessed | tf_op | source)
XLA Modules:
  0.0 119.1 jit_solution(6941959016429797838)
XLA Ops:
  0.6 1.3 %broadcast_in_dim.9.an_ref = bf16[1,2560]{1,0:T(2,128)(2,1)} reshape(bf16[2560]{0:T(1024)(128)(2,1)} %param.16) | data formatting | bytes 10240 | tf_op jit(solution)/shard_map/broadcast_in_dim | solution.py:114
  1.9 17.3 %project.1 = (bf16[8,256,256]{2,1,0:T(8,128)(2,1)}, bf16[8,2,64,128]{3,2,1,0:T(8,128)(2,1)}, bf16[8,2,64,128]{3,2,1,0:T(8,128)(2,1)}, bf16[8,128,128]{2,1,0:T(8,128)(2,1)}, bf16[8,128,128]{2,1,0:T(8,128)(2,1)}) custom-call(s32[8]{0:T(128)} %prefix_ref.3, bf16[512,2560]{1,0:T(8,128)(2,1)} %bitcast.9, bf16[1,2560]{1,0:T(2,128)(2,1)} %broadcast_in_dim.9.an_ref, ...), custom_call_target="tpu_custom_call" | custom-call | flops 4026531840 | bytes 12582912 | tf_op jit(solution)/shard_map/project/pallas_call | solution.py:98
  19.2 96.4 %attend_and_combine.1 = bf16[8,64,2560]{2,1,0:T(8,128)(2,1)} custom-call(s32[8]{0:T(128)} %prefix_ref.3, bf16[8,256,256]{2,1,0:T(8,128)(2,1)} %get-tuple-element.8.q_ref, bf16[8,8192,128]{2,1,0:T(8,128)(2,1)} %bitcast.7, bf16[8,8192,128]{2,1,0:T(8,128)(2,1)} %bitcast.8, bf16[8,2,64,128]{3,2,1,0:T(8,128)(2,1)} %get-tuple-element.9.k_own, ...), custom_call_target="tpu_custom_call" | custom-call | flops 20401094656 | bytes 48234496 | tf_op jit(solution)/shard_map/attend_and_combine/pallas_call | solution.py:503
  115.7 3.4 %copy.16 = bf16[8,64,2560]{2,1,0:T(8,128)(2,1)} copy(bf16[8,64,2560]{2,1,0:T(8,128)(2,1)} %attend_and_combine.1) | data formatting | bytes 5242880

commit v5 on v4

--- a/solution.py
+++ b/solution.py
@@ -36,7 +36,9 @@
                    q_ref, k_ref, v_ref, kn_out, vn_out, wq, wk, wv, normed, cos_ref, sin_ref, sems):
     n_seq, n_new = k_ref.shape[0], k_ref.shape[2]
     rows = n_seq * n_new
-    copies = [pltpu.make_async_copy(wq_hbm.at[:, pl.ds(256 * j, 256)], wq.at[j], sems.at[j]) for j in range(4)]
+    depth = wq.shape[0] // 4
+    copies = [pltpu.make_async_copy(wq_hbm.at[pl.ds(depth * j, depth)], wq.at[pl.ds(depth * j, depth)], sems.at[j])
+              for j in range(4)]
     copies.append(pltpu.make_async_copy(wk_hbm, wk, sems.at[4]))
     copies.append(pltpu.make_async_copy(wv_hbm, wv, sems.at[5]))
     for c in copies:
@@ -44,7 +46,9 @@
     for r in range(0, rows, 64):
         x = x_ref[r:r + 64, :].astype(F32)
         scale = lax.rsqrt(jnp.mean(x * x, axis=-1, keepdims=True) + EPS)
-        normed[r:r + 64, :] = (x * scale * an_ref[...].astype(F32)).astype(BF16)
+        for j in range(x.shape[1] // 128):
+            cols = slice(128 * j, 128 * j + 128)
+            normed[r:r + 64, cols] = (x[:, cols] * scale * an_ref[j:j + 1, :].astype(F32)).astype(BF16)
     low = lax.broadcasted_iota(jnp.int32, (n_new, HEAD_DIM), 1) < HEAD_DIM // 2
     step = lax.broadcasted_iota(jnp.int32, (n_new, HEAD_DIM), 0)
     for b in range(n_seq):
@@ -61,7 +65,8 @@
 
     for j in range(4):
         copies[j].wait()
-        y = jnp.dot(normed[...], wq[j], preferred_element_type=F32)
+    for j in range(4):
+        y = jnp.dot(normed[...], wq[:, 256 * j:256 * j + 256], preferred_element_type=F32)
         for i in range(2):
             h, g = j // 2, 2 * (j % 2) + i
             head = norm_rope(y[:, i * HEAD_DIM:(i + 1) * HEAD_DIM], qn_ref)
@@ -104,18 +109,18 @@
                    jax.ShapeDtypeStruct((n_seq, 2 * n_new, HEAD_DIM), BF16)),
         in_specs=[pl.BlockSpec(memory_space=pltpu.SMEM), vmem, vmem, hbm, hbm, hbm, vmem, vmem, vmem],
         out_specs=(vmem,) * 5,
-        scratch_shapes=[pltpu.VMEM((4, d_model, 256), BF16), pltpu.VMEM((d_model, 256), BF16),
+        scratch_shapes=[pltpu.VMEM(w_q.shape, BF16), pltpu.VMEM((d_model, 256), BF16),
                         pltpu.VMEM((d_model, 256), BF16), pltpu.VMEM((rows, d_model), BF16),
                         pltpu.VMEM((rows, HEAD_DIM), F32), pltpu.VMEM((rows, HEAD_DIM), F32),
                         pltpu.SemaphoreType.DMA((6,))],
         compiler_params=pltpu.CompilerParams(vmem_limit_bytes=VMEM_LIMIT),
         cost_estimate=pl.CostEstimate(flops=2 * rows * d_model * 1536, bytes_accessed=12 << 20, transcendentals=0),
         name="project",
-    )(prefix_len, hidden.reshape(rows, d_model), attn_norm[None], w_q, w_k, w_v, q_norm[None], k_norm[None], freq)
-
-
-CHUNK = 2048
-SLOTS = 4
+    )(prefix_len, hidden.reshape(rows, d_model), attn_norm.reshape(d_model // 128, 128), w_q, w_k, w_v, q_norm[None], k_norm[None], freq)
+
+
+CHUNK = 4096
+SLOTS = 3
 
 
 def pair_reduce(op, x):
@@ -123,8 +128,10 @@
     return op(x, pltpu.roll(x, 4, 0))
 
 
-def split_heads(x, par_ref):
-    return jnp.concatenate([x * par_ref[h] for h in range(2)], axis=1)
+def split_heads(x):
+    even = (lax.broadcasted_iota(jnp.int32, (16, HEAD_DIM), 0) % 2 == 0).astype(F32)
+    gains = [even.astype(BF16), (1.0 - even).astype(BF16)]
+    return jnp.concatenate([x * jnp.concatenate([g] * (x.shape[0] // 16), axis=0) for g in gains], axis=1)
 
 
 def own_keys(q, k_own_ref, v_own_ref):
@@ -145,16 +152,13 @@
     return (jnp.where(even, maxes[0], maxes[1]), jnp.where(even, sums[0], sums[1]), accs)
 
 
-def attend_step(it, n_seq, per_seq, limit_of, q_all, k_ref, v_ref, k_own, v_own, par_ref, emit,
+def attend_step(it, n_seq, per_seq, limit_of, q_all, k_ref, v_ref, k_own, v_own, emit,
                 s_a, s_b, m_ref, l_ref, acc_ref, m_own, l_own, acc_own):
     cp = lax.axis_index("cp")
     s_refs = (s_a, s_b)
 
     @pl.when(it == 0)
     def _():
-        even = (lax.broadcasted_iota(jnp.int32, (CHUNK, HEAD_DIM), 0) % 2 == 0).astype(F32)
-        par_ref[0] = even.astype(BF16)
-        par_ref[1] = (1.0 - even).astype(BF16)
         acc_ref[...] = jnp.zeros_like(acc_ref)
         l_ref[...] = jnp.zeros_like(l_ref)
 
@@ -178,7 +182,7 @@
     rows = pl.ds(pl.multiple_of(i * CHUNK, CHUNK), CHUNK)
 
     def score_dot():
-        both = split_heads(k_ref[...], par_ref)
+        both = split_heads(k_ref[...])
         return lax.dot_general(both, q_all[b_new], NT, preferred_element_type=F32)
 
     def score_post(s, par):
@@ -196,7 +200,7 @@
         return p.reshape(CHUNK, 256).astype(BF16)
 
     def value(p):
-        both = split_heads(v_ref[...], par_ref)
+        both = split_heads(v_ref[...])
         part = lax.dot_general(both, p, TN, preferred_element_type=F32)
         acc_ref[...] = jnp.where(i == 0, 0.0, acc_ref[...]) + part
 
@@ -270,12 +274,12 @@
 
 
 STAGES = 7
-PIECES = 5
-LAGS = (3, 7, 11, 15, 18, 22, 24)
+PIECES = 2
+LAGS = (2, 4, 6, 8, 9, 11, 12)
 
 
 def fused_kernel(prefix_ref, q_ref, k_hbm, v_hbm, k_own, v_own, x_hbm, wo_hbm, out_ref,
-                 par_ref, k_buf, v_buf, k_sem, v_sem, s_a, s_b, m_ref, l_ref, acc_ref, m_own, l_own, acc_own,
+                 k_buf, v_buf, k_sem, v_sem, s_a, s_b, m_ref, l_ref, acc_ref, m_own, l_own, acc_own,
                  part_ref, x_buf, wo, ra1, sa2, ra2, proj, rs_o, rs_i, fwd, og,
                  loc_sem, a1_s, a1_r, a2_s, a2_r, rs_s, rso_r, rsi_r, og_s, og_r):
     it = pl.program_id(0)
@@ -358,7 +362,7 @@
         a1(b).start()
 
     attend_step(it, n_seq, per_seq, lambda b: 2 * prefix_ref[b] - cp * (per_seq * CHUNK), q_ref, k_buf.at[it % SLOTS],
-                v_buf.at[it % SLOTS], k_own, v_own, par_ref, emit,
+                v_buf.at[it % SLOTS], k_own, v_own, emit,
                 s_a, s_b, m_ref, l_ref, acc_ref, m_own, l_own, acc_own)
 
     def s1(u):
@@ -385,8 +389,10 @@
                 cols = pl.ds(pl.multiple_of((half * pieces + p) * width, width), width)
                 proj[u, half, p] = jnp.dot(o, wo[:, cols], preferred_element_type=F32)
 
-                @pl.when(is_end)
-                def _(half=half, p=p):
+        @pl.when(is_end)
+        def _():
+            for half in (far, near):
+                for p in range(pieces):
                     rs_out(u, half, p).start()
 
     def s3(u):
@@ -507,7 +513,7 @@
         in_specs=[pl.BlockSpec(memory_space=pltpu.SMEM), vmem, hbm, hbm, vmem, vmem, hbm, hbm],
         out_specs=vmem,
         scratch_shapes=[
-            pltpu.VMEM((2, CHUNK, HEAD_DIM), BF16), pltpu.VMEM((SLOTS, CHUNK, HEAD_DIM), BF16),
+            pltpu.VMEM((SLOTS, CHUNK, HEAD_DIM), BF16),
             pltpu.VMEM((SLOTS, CHUNK, HEAD_DIM), BF16), dma((SLOTS,)), dma((SLOTS,)),
             pltpu.VMEM((slots * 2, 256), F32), pltpu.VMEM((slots * 2, 256), F32),
             pltpu.VMEM((2, 8, 256), F32), pltpu.VMEM((2, 8, 256), F32), pltpu.VMEM((256, 256), F32),
@@ -520,7 +526,7 @@
             pltpu.VMEM((units, PIECES, 32, width), F32), pltpu.VMEM((4, units, 2, PIECES, 32, width), F32),
             dma((1 + units,)), dma((n_seq,)), dma((n_seq,)), dma((units,)), dma((units,)), dma((units, 2, PIECES)),
             dma((units, 2, PIECES)), dma((units, PIECES)), dma((5, units, 2, PIECES)), dma((4, units, 2, PIECES))],
-        compiler_params=pltpu.CompilerParams(collective_id=0, has_side_effects=True, vmem_limit_bytes=56 << 20),
+        compiler_params=pltpu.CompilerParams(collective_id=0, has_side_effects=True, vmem_limit_bytes=VMEM_LIMIT),
         cost_estimate=pl.CostEstimate(flops=19 << 30, bytes_accessed=46 << 20, transcendentals=17 << 20),
         name="attend_and_combine",
     )(prefix_len, q, k_rows, v_rows, k_own, v_own, hidden, w_o)

time: 119 us -> 110 us (0.924)
  Pallas kernels: 114 us -> 105 us
  local copies, waits for them, and re-layouts: 4.69 us -> 3.4 us
    pallas_call x1, Pallas kernels: 96.4 us -> 91.5 us  [attend_and_combine(): pl.pallas_call(fused_kernel, grid=((n_seq + 1) * per_seq,), out_shape=jax...]
    pallas_call x1, Pallas kernels: 17.3 us -> 13.8 us  [project(): pl.pallas_call(project_kernel, out_shape=(jax.ShapeDtypeStruct((n_seq, 25...]
    broadcast_in_dim x1 -> x0, local copies, waits for them, and re-layouts: 1.29 us -> none  [project(): attn_norm[None]]
where the time goes in v5:
time: 110 us; the launch traced here: 109 us
  Pallas kernels  105 us (95%)
  local copies, waits for them, and re-layouts  3.4 us (3%)
    pallas_call x1, Pallas kernels, attend_and_combine(): pl.pallas_call(fused_kernel, grid=((n_seq + 1) * per_seq,), out_shape=jax...  91.5 us
    pallas_call x1, Pallas kernels, project(): pl.pallas_call(project_kernel, out_shape=(jax.ShapeDtypeStruct((n_seq, 25...  13.8 us
    unnamed x1, local copies, waits for them, and re-layouts  3.4 us

profile of v5, /device:TPU:0, one launch (start us, length us, event | category | flops | bytes accessed | tf_op | source)
XLA Modules:
  0.0 109.3 jit_solution(5648982066543499500)
XLA Ops:
  0.6 13.8 %project.1 = (bf16[8,256,256]{2,1,0:T(8,128)(2,1)}, bf16[8,2,64,128]{3,2,1,0:T(8,128)(2,1)}, bf16[8,2,64,128]{3,2,1,0:T(8,128)(2,1)}, bf16[8,128,128]{2,1,0:T(8,128)(2,1)}, bf16[8,128,128]{2,1,0:T(8,128)(2,1)}) custom-call(s32[8]{0:T(128)} %prefix_ref.3, bf16[512,2560]{1,0:T(8,128)(2,1)} %bitcast.10, bf16[20,128]{1,0:T(8,128)(2,1)} %bitcast.11, ...), custom_call_target="tpu_custom_call" | custom-call | flops 4026531840 | bytes 12582912 | tf_op jit(solution)/shard_map/project/pallas_call | solution.py:103
  14.4 91.5 %attend_and_combine.1 = bf16[8,64,2560]{2,1,0:T(8,128)(2,1)} custom-call(s32[8]{0:T(128)} %prefix_ref.3, bf16[8,256,256]{2,1,0:T(8,128)(2,1)} %get-tuple-element.8.q_ref, bf16[8,8192,128]{2,1,0:T(8,128)(2,1)} %bitcast.8, bf16[8,8192,128]{2,1,0:T(8,128)(2,1)} %bitcast.9, bf16[8,2,64,128]{3,2,1,0:T(8,128)(2,1)} %get-tuple-element.9.k_own, ...), custom_call_target="tpu_custom_call" | custom-call | flops 20401094656 | bytes 48234496 | tf_op jit(solution)/shard_map/attend_and_combine/pallas_call | solution.py:509
  105.9 3.4 %copy.16 = bf16[8,64,2560]{2,1,0:T(8,128)(2,1)} copy(bf16[8,64,2560]{2,1,0:T(8,128)(2,1)} %attend_and_combine.1) | data formatting | bytes 5242880

commit v6 on v5

--- a/solution.py
+++ b/solution.py
@@ -71,9 +71,9 @@
             h, g = j // 2, 2 * (j % 2) + i
             head = norm_rope(y[:, i * HEAD_DIM:(i + 1) * HEAD_DIM], qn_ref)
             for b in range(n_seq):
-                for c in range(2):
-                    q_ref[b, c * 128 + g * 32:c * 128 + g * 32 + 32, h * 128:(h + 1) * 128] = (
-                        head[b * 64 + c * 32:b * 64 + c * 32 + 32])
+                for part in range(4):
+                    q_ref[b, part * 64 + g * 16:part * 64 + g * 16 + 16, h * 128:(h + 1) * 128] = (
+                        head[b * 64 + part * 16:b * 64 + part * 16 + 16])
     dst = lax.broadcasted_iota(jnp.int32, (2 * n_new, 2 * n_new), 0)
     src = lax.broadcasted_iota(jnp.int32, (2 * n_new, 2 * n_new), 1)
     perm = (src == (dst % 2) * n_new + dst // 2).astype(F32).astype(BF16)
@@ -138,7 +138,7 @@
     n_new = k_own_ref.shape[-2]
     key = lax.broadcasted_iota(jnp.int32, (n_new, 256), 0)
     col = lax.broadcasted_iota(jnp.int32, (n_new, 256), 1)
-    keep = key <= (col // 128) * 32 + col % 32
+    keep = key <= (col // 64) * 16 + col % 16
     maxes, sums, accs = [], [], []
     for h in range(2):
         s = lax.dot_general(k_own_ref[h], q[:, h * 128:(h + 1) * 128], NT, preferred_element_type=F32)
@@ -268,25 +268,31 @@
     top = functools.reduce(jnp.maximum, maxes)
     weights = [jnp.exp2(m - top) for m in maxes]
     total = sum(w * s for w, s in zip(weights, stats))
-    stats_out = jnp.where(sub < 2, top, total)
     accs = [sum(w[h:h + 1] * p[h * 128:(h + 1) * 128, :] for w, p in zip(weights, parts)) for h in range(2)]
-    return accs, stats_out
-
-
-STAGES = 7
+    return accs, [top[h:h + 1] for h in range(2)], [total[2 + h:3 + h] for h in range(2)]
+
+
+def pack_half(pair, want):
+    first, second = pair
+    low = lax.broadcasted_iota(jnp.int32, first.shape, 1) < 64
+    at_zero = jnp.where(low, first, pltpu.roll(second, 64, 1))
+    at_one = jnp.where(low, pltpu.roll(first, 64, 1), second)
+    return jnp.where(want == 0, at_zero, at_one)
+
+
 PIECES = 2
-LAGS = (2, 4, 6, 8, 9, 11, 12)
+LAGS = (1, 3, 5, 6, 7, 9, 10)
 
 
 def fused_kernel(prefix_ref, q_ref, k_hbm, v_hbm, k_own, v_own, x_hbm, wo_hbm, out_ref,
                  k_buf, v_buf, k_sem, v_sem, s_a, s_b, m_ref, l_ref, acc_ref, m_own, l_own, acc_own,
-                 part_ref, x_buf, wo, ra1, sa2, ra2, proj, rs_o, rs_i, fwd, og,
+                 part_ref, x_buf, wo, ra1, sa2, oa2, ra2, proj, rs_o, rs_i, fwd, og,
                  loc_sem, a1_s, a1_r, a2_s, a2_r, rs_s, rso_r, rsi_r, og_s, og_r):
     it = pl.program_id(0)
     steps = pl.num_programs(0)
     per_seq = steps // (q_ref.shape[0] + 1)
     n_seq = q_ref.shape[0]
-    units = n_seq // 2
+    units = n_seq
     pieces, width = proj.shape[2], proj.shape[-1]
     cp, z = lax.axis_index("cp"), lax.axis_index("tp")
     y, c = cp // 2, cp % 2
@@ -305,7 +311,7 @@
                                             device_id=peer, device_id_type=MESH)
 
     wo_copy = pltpu.make_async_copy(wo_hbm, wo, loc_sem.at[0])
-    x_copies = [pltpu.make_async_copy(x_hbm.at[2 * u + y, pl.ds(32 * c, 32), :], x_buf.at[u], loc_sem.at[1 + u])
+    x_copies = [pltpu.make_async_copy(x_hbm.at[u, pl.ds(pl.multiple_of(32 * c + 16 * y, 16), 16), :], x_buf.at[u], loc_sem.at[1 + u])
                 for u in range(units)]
 
     @pl.when(it == 0)
@@ -366,24 +372,22 @@
                 s_a, s_b, m_ref, l_ref, acc_ref, m_own, l_own, acc_own)
 
     def s1(u):
-        b = 2 * u + 1 - y
-        a1(b).wait_recv()
-        accs, stats = merge([part_ref[b, c], ra1[b]])
-        for h in range(2):
-            sa2[u, h * 128:(h + 1) * 128, :] = accs[h]
-        sa2[u, 256:264, :] = stats
+        a1(u).wait_recv()
+        accs, tops, totals = merge([part_ref[u, c], ra1[u]])
+        for ref, want in ((sa2, 1 - y), (oa2, y)):
+            ref[u, 0:128, :] = pack_half(accs, want)
+            ref[u, 128:136, :] = jnp.broadcast_to(pack_half([jnp.broadcast_to(t, (8, 128)) for t in tops], want), (8, 128))
+            ref[u, 136:144, :] = jnp.broadcast_to(pack_half([jnp.broadcast_to(t, (8, 128)) for t in totals], want), (8, 128))
         a2(u).start()
 
     def s2(u):
-        b = 2 * u + y
-        a1(b).wait_recv()
         a2(u).wait_recv()
-        accs, stats = merge([part_ref[b, c], ra1[b], ra2[u]])
-        heads = []
-        for h in range(2):
-            o = (accs[h] / stats[2 + h:3 + h]).T.astype(BF16)
-            heads += [o[g * 32:(g + 1) * 32] for g in range(4)]
-        o = jnp.concatenate(heads, axis=1)
+        top = jnp.maximum(oa2[u, 128:136, :], ra2[u, 128:136, :])
+        weights = [jnp.exp2(ref[u, 128:136, :] - top) for ref in (oa2, ra2)]
+        total = weights[0] * oa2[u, 136:144, :] + weights[1] * ra2[u, 136:144, :]
+        o = weights[0][0:1] * oa2[u, 0:128, :] + weights[1][0:1] * ra2[u, 0:128, :]
+        o = (o / total[0:1]).T
+        o = jnp.concatenate([o[16 * i:16 * i + 16].astype(BF16) for i in range(8)], axis=1)
         for half in (far, near):
             for p in range(pieces):
                 cols = pl.ds(pl.multiple_of((half * pieces + p) * width, width), width)
@@ -441,7 +445,8 @@
 
     def put(q, u, half, p):
         cols = pl.ds(pl.multiple_of((half * pieces + p) * width, width), width)
-        out_ref[2 * u + q // 2, pl.ds(pl.multiple_of(32 * (q % 2), 32), 32), cols] = og[q, u, half, p].astype(BF16)
+        rows = pl.ds(pl.multiple_of(32 * (q % 2) + 16 * (q // 2), 16), 16)
+        out_ref[u, rows, cols] = og[q, u, half, p].astype(BF16)
 
     def s7(u):
         for half in (near, far):
@@ -458,13 +463,13 @@
 
     def slot(t, carry):
         for stage, lag in zip(stages, LAGS):
-            since = t - (3 * per_seq - 1) - lag
-            @pl.when(jnp.logical_and(since >= 0, jnp.logical_and(since < 2 * per_seq * units, since % (2 * per_seq) == 0)))
+            since = t - (2 * per_seq - 1) - lag
+            @pl.when(jnp.logical_and(since >= 0, jnp.logical_and(since < per_seq * units, since % per_seq == 0)))
             def _(stage=stage, since=since):
-                stage(since // (2 * per_seq))
+                stage(since // per_seq)
         return carry
 
-    last = (2 * units + 1) * per_seq - 1 + LAGS[-1]
+    last = (units + 1) * per_seq - 1 + LAGS[-1]
     lax.fori_loop(it, jnp.where(it == steps - 1, last + 1, it + 1), slot, 0)
 
     @pl.when(it == steps - 1)
@@ -502,7 +507,7 @@
     k_rows = k_cache.reshape(n_seq, slots * 2, HEAD_DIM)
     v_rows = v_cache.reshape(n_seq, slots * 2, HEAD_DIM)
     per_seq = slots * 2 // CHUNK
-    units, width = n_seq // 2, d_model // (2 * PIECES)
+    units, width = n_seq, d_model // (2 * PIECES)
     vmem = pl.BlockSpec(memory_space=pltpu.VMEM)
     hbm = pl.BlockSpec(memory_space=pl.ANY)
     dma = pltpu.SemaphoreType.DMA
@@ -519,11 +524,11 @@
             pltpu.VMEM((2, 8, 256), F32), pltpu.VMEM((2, 8, 256), F32), pltpu.VMEM((256, 256), F32),
             pltpu.VMEM((n_seq, 8, 256), F32), pltpu.VMEM((n_seq, 8, 256), F32), pltpu.VMEM((n_seq, 256, 256), F32),
             pltpu.VMEM((n_seq, 2, 264, 128), F32),
-            pltpu.VMEM((units, 32, d_model), BF16), pltpu.VMEM(w_o.shape, BF16),
-            pltpu.VMEM((n_seq, 264, 128), F32), pltpu.VMEM((units, 264, 128), F32),
-            pltpu.VMEM((units, 264, 128), F32), pltpu.VMEM((units, 2, PIECES, 32, width), F32),
-            pltpu.VMEM((units, 2, PIECES, 32, width), F32), pltpu.VMEM((units, PIECES, 32, width), F32),
-            pltpu.VMEM((units, PIECES, 32, width), F32), pltpu.VMEM((4, units, 2, PIECES, 32, width), F32),
+            pltpu.VMEM((units, 16, d_model), BF16), pltpu.VMEM(w_o.shape, BF16),
+            pltpu.VMEM((n_seq, 264, 128), F32), pltpu.VMEM((units, 144, 128), F32),
+            pltpu.VMEM((units, 144, 128), F32), pltpu.VMEM((units, 144, 128), F32), pltpu.VMEM((units, 2, PIECES, 16, width), F32),
+            pltpu.VMEM((units, 2, PIECES, 16, width), F32), pltpu.VMEM((units, PIECES, 16, width), F32),
+            pltpu.VMEM((units, PIECES, 16, width), F32), pltpu.VMEM((4, units, 2, PIECES, 16, width), F32),
             dma((1 + units,)), dma((n_seq,)), dma((n_seq,)), dma((units,)), dma((units,)), dma((units, 2, PIECES)),
             dma((units, 2, PIECES)), dma((units, PIECES)), dma((5, units, 2, PIECES)), dma((4, units, 2, PIECES))],
         compiler_params=pltpu.CompilerParams(collective_id=0, has_side_effects=True, vmem_limit_bytes=VMEM_LIMIT),

time: 110 us -> 107 us (0.973)
  Pallas kernels: 105 us -> 103 us
    pallas_call x1, Pallas kernels: 91.5 us -> 88.8 us  [attend_and_combine(): pl.pallas_call(fused_kernel, grid=((n_seq + 1) * per_seq,), out_shape=jax...]
where the time goes in v6:
time: 107 us
  Pallas kernels  103 us (96%)
  local copies, waits for them, and re-layouts  3.4 us (3%)
    pallas_call x1, Pallas kernels, attend_and_combine(): pl.pallas_call(fused_kernel, grid=((n_seq + 1) * per_seq,), out_shape=jax...  88.8 us
    pallas_call x1, Pallas kernels, project(): pl.pallas_call(project_kernel, out_shape=(jax.ShapeDtypeStruct((n_seq, 25...  13.8 us
    unnamed x1, local copies, waits for them, and re-layouts  3.4 us

profile of v6, /device:TPU:0, one launch (start us, length us, event | category | flops | bytes accessed | tf_op | source)
XLA Modules:
  0.0 106.6 jit_solution(10274587720632095439)
XLA Ops:
  0.6 13.8 %project.1 = (bf16[8,256,256]{2,1,0:T(8,128)(2,1)}, bf16[8,2,64,128]{3,2,1,0:T(8,128)(2,1)}, bf16[8,2,64,128]{3,2,1,0:T(8,128)(2,1)}, bf16[8,128,128]{2,1,0:T(8,128)(2,1)}, bf16[8,128,128]{2,1,0:T(8,128)(2,1)}) custom-call(s32[8]{0:T(128)} %prefix_ref.3, bf16[512,2560]{1,0:T(8,128)(2,1)} %bitcast.10, bf16[20,128]{1,0:T(8,128)(2,1)} %bitcast.11, ...), custom_call_target="tpu_custom_call" | custom-call | flops 4026531840 | bytes 12582912 | tf_op jit(solution)/shard_map/project/pallas_call | solution.py:103
  14.4 88.8 %attend_and_combine.1 = bf16[8,64,2560]{2,1,0:T(8,128)(2,1)} custom-call(s32[8]{0:T(128)} %prefix_ref.3, bf16[8,256,256]{2,1,0:T(8,128)(2,1)} %get-tuple-element.8.q_ref, bf16[8,8192,128]{2,1,0:T(8,128)(2,1)} %bitcast.8, bf16[8,8192,128]{2,1,0:T(8,128)(2,1)} %bitcast.9, bf16[8,2,64,128]{3,2,1,0:T(8,128)(2,1)} %get-tuple-element.9.k_own, ...), custom_call_target="tpu_custom_call" | custom-call | flops 20401094656 | bytes 48234496 | tf_op jit(solution)/shard_map/attend_and_combine/pallas_call | solution.py:514
  103.2 3.4 %copy.16 = bf16[8,64,2560]{2,1,0:T(8,128)(2,1)} copy(bf16[8,64,2560]{2,1,0:T(8,128)(2,1)} %attend_and_combine.1) | data formatting | bytes 5242880

commit v7 on v6

--- a/solution.py
+++ b/solution.py
@@ -281,7 +281,7 @@
 
 
 PIECES = 2
-LAGS = (1, 3, 5, 6, 7, 9, 10)
+LAGS = (1, 3, 8, 10, 13, 16, 18)
 
 
 def fused_kernel(prefix_ref, q_ref, k_hbm, v_hbm, k_own, v_own, x_hbm, wo_hbm, out_ref,
@@ -380,24 +380,32 @@
             ref[u, 136:144, :] = jnp.broadcast_to(pack_half([jnp.broadcast_to(t, (8, 128)) for t in totals], want), (8, 128))
         a2(u).start()
 
-    def s2(u):
+    def rows_of(u):
         a2(u).wait_recv()
         top = jnp.maximum(oa2[u, 128:136, :], ra2[u, 128:136, :])
         weights = [jnp.exp2(ref[u, 128:136, :] - top) for ref in (oa2, ra2)]
         total = weights[0] * oa2[u, 136:144, :] + weights[1] * ra2[u, 136:144, :]
         o = weights[0][0:1] * oa2[u, 0:128, :] + weights[1][0:1] * ra2[u, 0:128, :]
         o = (o / total[0:1]).T
-        o = jnp.concatenate([o[16 * i:16 * i + 16].astype(BF16) for i in range(8)], axis=1)
-        for half in (far, near):
-            for p in range(pieces):
-                cols = pl.ds(pl.multiple_of((half * pieces + p) * width, width), width)
-                proj[u, half, p] = jnp.dot(o, wo[:, cols], preferred_element_type=F32)
-
-        @pl.when(is_end)
-        def _():
+        return jnp.concatenate([o[16 * i:16 * i + 16].astype(BF16) for i in range(8)], axis=1)
+
+    def s2(u):
+        @pl.when(u % 2 == 1)
+        def _():
+            o = jnp.concatenate([rows_of(u - 1), rows_of(u)], axis=0)
             for half in (far, near):
                 for p in range(pieces):
-                    rs_out(u, half, p).start()
+                    cols = pl.ds(pl.multiple_of((half * pieces + p) * width, width), width)
+                    out = jnp.dot(o, wo[:, cols], preferred_element_type=F32)
+                    proj[u - 1, half, p] = out[0:16]
+                    proj[u, half, p] = out[16:32]
+
+            @pl.when(is_end)
+            def _():
+                for v in (u - 1, u):
+                    for half in (far, near):
+                        for p in range(pieces):
+                            rs_out(v, half, p).start()
 
     def s3(u):
         @pl.when(is_mid)

time: 107 us -> 101 us (0.944)
  Pallas kernels: 103 us -> 96.7 us
    pallas_call x1, Pallas kernels: 88.8 us -> 83 us  [attend_and_combine(): pl.pallas_call(fused_kernel, grid=((n_seq + 1) * per_seq,), out_shape=jax...]
where the time goes in v7:
time: 101 us
  Pallas kernels  96.7 us (96%)
  local copies, waits for them, and re-layouts  3.4 us (3%)
    pallas_call x1, Pallas kernels, attend_and_combine(): pl.pallas_call(fused_kernel, grid=((n_seq + 1) * per_seq,), out_shape=jax...  83 us
    pallas_call x1, Pallas kernels, project(): pl.pallas_call(project_kernel, out_shape=(jax.ShapeDtypeStruct((n_seq, 25...  13.8 us
    unnamed x1, local copies, waits for them, and re-layouts  3.4 us

profile of v7, /device:TPU:0, one launch (start us, length us, event | category | flops | bytes accessed | tf_op | source)
XLA Modules:
  0.0 100.8 jit_solution(6339684010149802357)
XLA Ops:
  0.6 13.8 %project.1 = (bf16[8,256,256]{2,1,0:T(8,128)(2,1)}, bf16[8,2,64,128]{3,2,1,0:T(8,128)(2,1)}, bf16[8,2,64,128]{3,2,1,0:T(8,128)(2,1)}, bf16[8,128,128]{2,1,0:T(8,128)(2,1)}, bf16[8,128,128]{2,1,0:T(8,128)(2,1)}) custom-call(s32[8]{0:T(128)} %prefix_ref.3, bf16[512,2560]{1,0:T(8,128)(2,1)} %bitcast.10, bf16[20,128]{1,0:T(8,128)(2,1)} %bitcast.11, ...), custom_call_target="tpu_custom_call" | custom-call | flops 4026531840 | bytes 12582912 | tf_op jit(solution)/shard_map/project/pallas_call | solution.py:103
  14.4 83.0 %attend_and_combine.1 = bf16[8,64,2560]{2,1,0:T(8,128)(2,1)} custom-call(s32[8]{0:T(128)} %prefix_ref.3, bf16[8,256,256]{2,1,0:T(8,128)(2,1)} %get-tuple-element.8.q_ref, bf16[8,8192,128]{2,1,0:T(8,128)(2,1)} %bitcast.8, bf16[8,8192,128]{2,1,0:T(8,128)(2,1)} %bitcast.9, bf16[8,2,64,128]{3,2,1,0:T(8,128)(2,1)} %get-tuple-element.9.k_own, ...), custom_call_target="tpu_custom_call" | custom-call | flops 20401094656 | bytes 48234496 | tf_op jit(solution)/shard_map/attend_and_combine/pallas_call | solution.py:522
  97.4 3.4 %copy.16 = bf16[8,64,2560]{2,1,0:T(8,128)(2,1)} copy(bf16[8,64,2560]{2,1,0:T(8,128)(2,1)} %attend_and_combine.1) | data formatting | bytes 5242880
